TPU v7x, 32 devices: a whole 2x2x4 slice. The times are simulated.
32 devices in a mesh: grp: 8 (over z, y), lane: 4 (over x, core).
Axes of the slice: x: 2, y: 2, z: 4, core: 2. Of those that a mesh axis runs over, the one named last changes fastest.
Arguments:
- grad_pooled: bfloat16 [4096, 16, 256], P(('grp', 'lane')), may hold values from -16 to 16
- bag_len: int32 [4096, 16], P(('grp', 'lane')), may hold values from 1 to 8
- lookup_slot: int32 [4096, 16, 8], P('grp', 'lane'), may hold values from -1 to 15, as said below
- slot_row: int32 [8, 4, 8, 2], P('grp', 'lane'), may hold values from 0 to 1023, as said below
- weights: float32 [16, 2048, 256], P('lane', 'grp'), may hold values from -6 to 6
- accum: float32 [16, 2048], P('lane', 'grp'), may hold values from 0.05 to 0.5
Outputs:
- new_weights: float32 [16, 2048, 256], P('lane', 'grp')
- new_accum: float32 [16, 2048], P('lane', 'grp')
Inputs may be any that keep to these rules, and one draw needn't show every extreme that they name: `lookup_slot`: position j of bag (b, t) holds -1 when j >= bag_len[b, t] and otherwise a slot number s; the row slot_row[s // 2, t // 4, g, s % 2], with g the group of sample b, lies in local table t % 4. `slot_row`: several slots, also from different groups, may name the same row.
All inputs are finite; a program needn't handle non-finite values.
Results may differ from a plain program's by a relative error of at most 0.0035.
Values may be sent and summed in bfloat16 or wider, within the bound.
A program may use at most 64 MiB of HBM per device.

v0:
```python
import functools
import math

import jax
import jax.numpy as jnp
from jax import lax
from jax.experimental import pallas as pl
from jax.experimental.pallas import tpu as pltpu
from jax.sharding import PartitionSpec as P

MESH = pl.DeviceIdType.MESH
LEARN_RATE = 0.3
EPSILON = 1e-06
F32 = jnp.float32
BF16 = jnp.bfloat16


def each(count, body):
    if count <= 64:
        for i in range(count):
            body(i)
    else:

        def step(i, carry):
            body(i)
            return carry

        lax.fori_loop(0, count, step, 0)


def iota(shape, dim):
    return lax.broadcasted_iota(jnp.int32, shape, dim)


def kernel(
    groups,
    lanes,
    place_base,
    accum_base,
    grad_hbm,
    len_hbm,
    look_hbm,
    slot_hbm,
    accum_hbm,
    packed,
    grad_in,
    grad_f32,
    grad_t,
    len_v,
    marks,
    marks_in,
    marks_out,
    slot_v,
    accum_v,
    part,
    recv,
    incoming,
    norm_out,
    norm_in,
    load_sem,
    look_sem,
    a_send,
    a_recv,
    b_send,
    b_recv,
    c_send,
    c_recv,
):
    devices = groups * lanes
    per_peer, embed = recv.shape[1], recv.shape[2]
    slots = groups * per_peer
    tables_all, batch = grad_t.shape[0], grad_t.shape[1]
    tables = tables_all // lanes
    depth = marks.shape[2]
    rows = accum_v.shape[1]
    grp = lax.axis_index("grp")
    lane = lax.axis_index("lane")
    me = grp * lanes + lane
    sign = 2 * (grp // (groups // 2)) - 1

    lane_steps = [(dx, dc) for dx in range(lanes // 2) for dc in range(2)]

    def lane_peer(step, sign):
        dx, dc = step
        half = lanes // 2
        chip = (lane // 2 + sign * dx + half) % half
        return chip * 2 + (lane % 2 + dc) % 2

    def partial_of(m):
        highs, lows = [], []
        for t in range(tables):
            mark = marks[m, t].astype(F32)
            count = jnp.zeros((slots, batch), F32)
            for j in range(depth):
                count += jnp.where(mark[j : j + 1, :] == number, 1.0, 0.0)
            length = len_v[pl.ds(m * tables + t, 1), :].astype(F32)
            factor = count / length
            high = factor.astype(BF16)
            highs.append(high)
            lows.append((factor - high.astype(F32)).astype(BF16))
        factors = jnp.concatenate(
            [jnp.concatenate(highs, axis=1), jnp.concatenate(lows, axis=1)], axis=0
        )
        values = grad_t[pl.ds(m * tables, tables)].reshape(tables * batch, embed)
        both = jnp.dot(factors, values, preferred_element_type=F32)
        return both[:slots] + both[slots:]

    barrier = pltpu.get_barrier_semaphore()

    def greet(i):
        far = (me + sign * (i + 1) + devices) % devices
        pl.semaphore_signal(
            barrier, inc=1, device_id=(far // lanes, far % lanes), device_id_type=MESH
        )

    look_copies = []
    for k, step in enumerate(lane_steps):
        q = lane_peer(step, 1)
        src = look_hbm.at[:, :, pl.ds(pl.multiple_of(q * batch, batch), batch)]
        look_copies.append(pltpu.make_async_copy(src, marks_in.at[k], look_sem.at[k]))
        look_copies[-1].start()
    grad_copy = pltpu.make_async_copy(grad_hbm, grad_in, load_sem.at[0])
    grad_copy.start()
    if devices <= 64:
        for i in range(devices - 1):
            greet(i)
    else:
        each(devices - 1, greet)
    small_copies = [
        pltpu.make_async_copy(len_hbm, len_v, load_sem.at[1]),
        pltpu.make_async_copy(slot_hbm, slot_v, load_sem.at[2]),
        pltpu.make_async_copy(accum_hbm, accum_v, load_sem.at[3]),
    ]
    for copy in small_copies:
        copy.start()
    for copy in look_copies:
        copy.wait()
    for k in range(1, lanes):
        marks_out[k - 1] = marks_in[k].astype(F32).astype(marks_out.dtype)
    pl.semaphore_wait(barrier, devices - 1)

    a_copies = []
    for k, step in enumerate(lane_steps[1:], 1):
        copy = pltpu.make_async_remote_copy(
            src_ref=marks_out.at[k - 1],
            dst_ref=marks.at[lane],
            send_sem=a_send.at[k - 1],
            recv_sem=a_recv.at[k - 1],
            device_id=(grp, lane_peer(step, 1)),
            device_id_type=MESH,
        )
        copy.start()
        a_copies.append(copy)

    grad_copy.wait()
    for c in range(embed // 128):
        grad_f32[c] = grad_in[:, c * 128 : (c + 1) * 128].astype(F32)
    for t in range(tables_all):
        for c in range(embed // 128):
            grad_t[t, :, c * 128 : (c + 1) * 128] = grad_f32[
                c, pl.ds(t, batch, stride=tables_all), :
            ].astype(BF16)
    for copy in small_copies:
        copy.wait()

    marks[lane] = marks_in[0].astype(F32).astype(marks.dtype)
    number = iota((slots, batch), 0).astype(F32)
    far_first = list(range(1, groups)) + [0]

    for k, step in enumerate(lane_steps):
        m = lane_peer(step, -1)
        if k > 0:
            a_copies[k - 1].wait_recv()
        total = partial_of(m)
        for p in range(groups):
            part[m, p] = total[p * per_peer : (p + 1) * per_peer].astype(BF16)

        def send(p):
            pltpu.make_async_remote_copy(
                src_ref=part.at[m, p],
                dst_ref=recv.at[me],
                send_sem=b_send,
                recv_sem=b_recv,
                device_id=(p, m),
                device_id_type=MESH,
            ).start()

        if groups <= 64:
            for dp in far_first:
                if k == 0 and dp == 0:
                    pltpu.make_async_copy(part.at[m, grp], recv.at[me], b_recv).start()
                else:
                    send((grp + sign * dp + groups) % groups)
        else:
            each(groups - 1, lambda i: send((grp + i + 1) % groups))
            if k == 0:
                pltpu.make_async_copy(part.at[m, grp], recv.at[me], b_recv).start()
            else:
                send(grp)

    slot_f = slot_v[...].astype(F32)
    which = iota((slots, groups), 0)
    column_pick = jnp.zeros((slots, groups), F32)
    for k in range(per_peer):
        column_pick = jnp.where(which % per_peer == k, slot_f[k : k + 1, :], column_pick)
    column_pick = jnp.where(which // per_peer == iota((slots, groups), 1), column_pick, 0.0)
    target_col = jnp.sum(column_pick, axis=1, keepdims=True)
    i_id, j_id = iota((slots, slots), 0), iota((slots, slots), 1)
    target_row = jnp.sum(jnp.where(i_id == j_id, target_col, 0.0), axis=0, keepdims=True)
    same = target_col == target_row
    first_col = jnp.sum(jnp.where(same & (j_id < i_id), 1.0, 0.0), axis=1, keepdims=True) == 0.0
    first_row = jnp.sum(jnp.where(same & (i_id < j_id), 1.0, 0.0), axis=0, keepdims=True) == 0.0
    place_row = jnp.where(first_row, target_row, -1.0)
    packed[place_base : place_base + 1, :slots] = place_row
    same_w = jnp.where(same, 1.0, 0.0).astype(BF16)

    hits = []
    accum_col = jnp.zeros((slots, 1), F32)
    for t in range(tables):
        hit = target_col == (iota((slots, rows), 1) + t * rows).astype(F32)
        hits.append(hit)
        accum_col += jnp.sum(
            jnp.where(hit, accum_v[t : t + 1, :], 0.0), axis=1, keepdims=True
        )

    pltpu.make_async_copy(recv, recv, b_recv).wait()
    for g in range(groups):
        group_sum = recv[g * lanes].astype(F32)
        for q in range(1, lanes):
            group_sum += recv[g * lanes + q].astype(F32)
        incoming[g * per_peer : (g + 1) * per_peer, :] = group_sum
    grads = jnp.dot(same_w, incoming[...].astype(BF16), preferred_element_type=F32)
    square_col = jnp.sum(grads * grads, axis=1, keepdims=True) * (1.0 / embed)
    square_first = jnp.where(first_col, square_col, 0.0)
    local = embed * jnp.sum(square_first, axis=0, keepdims=True)
    norm_out[...] = jnp.broadcast_to(local, (1, 128))

    def tell(far):
        pltpu.make_async_remote_copy(
            src_ref=norm_out,
            dst_ref=norm_in.at[me],
            send_sem=c_send,
            recv_sem=c_recv,
            device_id=(far // lanes, far % lanes),
            device_id_type=MESH,
        ).start()

    if devices <= 64:
        for d in range(1, devices):
            tell((me + sign * d + devices) % devices)
    else:
        each(devices - 1, lambda i: tell((me + i + 1) % devices))
    pltpu.make_async_copy(norm_out, norm_in.at[me], c_recv).start()

    square_rows = [
        jnp.sum(jnp.where(hit, square_first, 0.0), axis=0, keepdims=True) for hit in hits
    ]
    for copy in a_copies:
        copy.wait_send()
    sent = recv.at[pl.ds(0, devices - 1)]
    pltpu.make_async_copy(sent, sent, b_send).wait()

    pltpu.make_async_copy(norm_in, norm_in, c_recv).wait()
    norm_total = jnp.sum(norm_in[...], axis=0)[:, :1]
    clip_limit = 0.5 * math.sqrt(devices * slots * embed)
    clip = clip_limit / jnp.maximum(jnp.sqrt(norm_total), clip_limit)
    for t in range(tables):
        packed[accum_base + t : accum_base + t + 1, :rows] = accum_v[t : t + 1, :] + clip * clip * square_rows[t]
    new_accum_col = accum_col + clip * clip * square_col
    delta = LEARN_RATE * clip * grads / (jnp.sqrt(new_accum_col) + EPSILON)
    packed[:slots, :embed] = delta
    told = norm_in.at[pl.ds(0, devices - 1)]
    pltpu.make_async_copy(told, told, c_send).wait()


def update_kernel(
    chunk, slots, place_base, accum_base, weights, packed, wout, aout, held, accum, sems, accum_sem
):
    accum[...] = packed[accum_base : accum_base + accum.shape[0], : accum.shape[1]]
    accum_copy = pltpu.make_async_copy(accum, aout, accum_sem)
    accum_copy.start()
    delta = packed[:slots, : weights.shape[2]]
    high = delta.astype(BF16)
    deltas = jnp.concatenate([high, (delta - high.astype(F32)).astype(BF16)], axis=0)
    place_row = packed[place_base : place_base + 1, :slots]
    place_row = jnp.concatenate([place_row, place_row], axis=1)
    tables, rows = weights.shape[0], weights.shape[1]
    copies = []
    for t in range(tables):
        for c in range(0, rows, chunk):
            row_id = (iota((chunk, 1), 0) + (t * rows + c)).astype(F32)
            place = jnp.where(row_id == place_row, 1.0, 0.0).astype(BF16)
            held[t, c : c + chunk] = weights[t, c : c + chunk] - jnp.dot(
                place, deltas, preferred_element_type=F32
            )
            copies.append(
                pltpu.make_async_copy(
                    held.at[t, pl.ds(c, chunk)],
                    wout.at[t, pl.ds(c, chunk)],
                    sems.at[len(copies)],
                )
            )
            copies[-1].start()
    for copy in copies:
        copy.wait()
    accum_copy.wait()


def per_device(groups, lanes, grad_pooled, bag_len, lookup_slot, slot_row, weights, accum):
    batch, tables_all, embed = grad_pooled.shape
    samples, tables, depth = lookup_slot.shape
    rows = accum.shape[1]
    per_peer = slot_row.shape[3]
    devices = groups * lanes
    slots = groups * per_peer
    mark_type = BF16 if slots <= 256 else F32
    place_base = -(-slots // 8) * 8
    accum_base = place_base + 8
    packed_shape = (accum_base + -(-tables // 8) * 8, max(embed, rows, slots))
    anywhere = pl.BlockSpec(memory_space=pl.ANY)
    vmem = pl.BlockSpec(memory_space=pltpu.VMEM)
    packed = pl.pallas_call(
        functools.partial(kernel, groups, lanes, place_base, accum_base),
        out_shape=jax.ShapeDtypeStruct(packed_shape, F32),
        in_specs=[pl.BlockSpec(memory_space=pltpu.HBM)] * 5,
        out_specs=vmem,
        cost_estimate=pl.CostEstimate(
            flops=8 * slots * batch * tables_all * embed,
            bytes_accessed=32 * batch * tables_all * embed,
            transcendentals=0,
        ),
        scratch_shapes=[
            pltpu.VMEM((batch * tables_all, embed), BF16),
            pltpu.VMEM((embed // 128, batch * tables_all, 128), F32),
            pltpu.VMEM((tables_all, batch, embed), BF16),
            pltpu.VMEM((tables_all, batch), jnp.int32),
            pltpu.VMEM((lanes, tables, depth, batch), mark_type),
            pltpu.VMEM((lanes, tables, depth, batch), jnp.int32),
            pltpu.VMEM((lanes - 1, tables, depth, batch), mark_type),
            pltpu.VMEM((per_peer, groups), jnp.int32),
            pltpu.VMEM((tables, rows), F32),
            pltpu.VMEM((lanes, groups, per_peer, embed), BF16),
            pltpu.VMEM((devices, per_peer, embed), BF16),
            pltpu.VMEM((slots, embed), F32),
            pltpu.VMEM((1, 128), F32),
            pltpu.VMEM((devices, 1, 128), F32),
            pltpu.SemaphoreType.DMA((4,)),
            pltpu.SemaphoreType.DMA((lanes,)),
            pltpu.SemaphoreType.DMA((lanes - 1,)),
            pltpu.SemaphoreType.DMA((lanes - 1,)),
            pltpu.SemaphoreType.DMA,
            pltpu.SemaphoreType.DMA,
            pltpu.SemaphoreType.DMA,
            pltpu.SemaphoreType.DMA,
        ],
        compiler_params=pltpu.CompilerParams(
            collective_id=0, has_side_effects=True
        ),
    )(
        grad_pooled.reshape(batch * tables_all, embed),
        bag_len.T,
        jnp.transpose(lookup_slot, (1, 2, 0)),
        slot_row.reshape(groups, per_peer).T,
        accum,
    )
    chunk = min(rows, 128)
    return pl.pallas_call(
        functools.partial(update_kernel, chunk, slots, place_base, accum_base),
        out_shape=(
            jax.ShapeDtypeStruct(weights.shape, F32),
            jax.ShapeDtypeStruct(accum.shape, F32),
        ),
        in_specs=[vmem, vmem],
        out_specs=(anywhere, anywhere),
        scratch_shapes=[
            pltpu.VMEM(weights.shape, F32),
            pltpu.VMEM(accum.shape, F32),
            pltpu.SemaphoreType.DMA((tables * (rows // chunk),)),
            pltpu.SemaphoreType.DMA,
        ],
        compiler_params=pltpu.CompilerParams(vmem_limit_bytes=8 << 20),
    )(weights, packed)


def solution(mesh):
    placed = (
        P(("grp", "lane"), None, None),
        P(("grp", "lane"), None),
        P("grp", "lane", None),
        P("grp", "lane", None, None),
        P("lane", "grp", None),
        P("lane", "grp"),
    )
    return jax.shard_map(
        functools.partial(per_device, mesh.shape["grp"], mesh.shape["lane"]),
        mesh=mesh,
        in_specs=placed,
        out_specs=(P("lane", "grp", None), P("lane", "grp")),
        check_vma=False,
    )
```

profile of v0, /device:TPU:0, one launch (start us, length us, event | category | flops | bytes accessed | tf_op | source)
XLA Modules:
  0.0 22.0 jit_solution(12949965207628892534)
XLA Ops:
  0.6 0.0 copy-start
  0.6 19.3 %shard_map.77.packed = f32[32,256]{1,0:T(8,128)} custom-call(bf16[2048,256]{1,0:T(8,128)(2,1)} %bitcast.6, s32[16,128]{1,0:T(8,128)} %bitcast.8, s32[4,8,512]{2,1,0:T(8,128)} %bitcast.7, s32[2,8]{1,0:T(2,128)} %bitcast.9, f32[4,256]{1,0:T(4,128)} %accum_hbm.1), custom_call_target="tpu_custom_call" | custom-call | flops 67108864 | bytes 16777216 | tf_op jit(solution)/shard_map/pallas_call | solution.py:322
  19.9 0.0 copy-done
  20.0 0.0 copy-start.1
  20.0 0.7 %copy-done.1 = f32[32,256]{1,0:T(8,128)S(1)} copy-done((f32[32,256]{1,0:T(8,128)S(1)}, f32[32,256]{1,0:T(8,128)}, u32[]{:S(2)}) %copy-start.1) | copy-done | bytes 32792
  20.7 1.3 %shard_map.78 = (f32[4,256,256]{2,1,0:T(8,128)}, f32[4,256]{1,0:T(4,128)}) custom-call(f32[4,256,256]{2,1,0:T(8,128)S(1)} %copy-done, f32[32,256]{1,0:T(8,128)S(1)} %copy-done.1), custom_call_target="tpu_custom_call" | custom-call | tf_op jit(solution)/shard_map/pallas_call | solution.py:367
Async XLA Ops:
  0.6 19.3 %copy-start = (f32[4,256,256]{2,1,0:T(8,128)S(1)}, f32[4,256,256]{2,1,0:T(8,128)}, u32[]{:S(2)}) copy-start(f32[4,256,256]{2,1,0:T(8,128)} %weights.1) | copy-start | bytes 3145732
  20.0 0.8 %copy-start.1 = (f32[32,256]{1,0:T(8,128)S(1)}, f32[32,256]{1,0:T(8,128)}, u32[]{:S(2)}) copy-start(f32[32,256]{1,0:T(8,128)} %shard_map.77.packed) | copy-start | bytes 98308
where the time goes:
time: 22.2 us; the launch traced here: 22 us
  Pallas kernels  20.6 us (93%)
  local copies, waits for them, and re-layouts  0.76 us (3%)
  between operations  0.66 us (3%)
    pallas_call x1, Pallas kernels, per_device(): pl.pallas_call(functools.partial(kernel, groups, lanes, place_base, accum...  19.3 us
    pallas_call x1, Pallas kernels, per_device(): pl.pallas_call(functools.partial(update_kernel, chunk, slots, place_base,...  1.28 us
    unnamed x4, local copies, waits for them, and re-layouts  0.76 us

commit v1 on v0

--- a/solution.py
+++ b/solution.py
@@ -354,14 +354,19 @@
             pltpu.SemaphoreType.DMA,
         ],
         compiler_params=pltpu.CompilerParams(
-            collective_id=0, has_side_effects=True
+            collective_id=0, has_side_effects=True, vmem_limit_bytes=32 << 20
         ),
     )(
-        grad_pooled.reshape(batch * tables_all, embed),
-        bag_len.T,
-        jnp.transpose(lookup_slot, (1, 2, 0)),
-        slot_row.reshape(groups, per_peer).T,
-        accum,
+        *(
+            pltpu.with_memory_space_constraint(operand, pltpu.HBM)
+            for operand in (
+                grad_pooled.reshape(batch * tables_all, embed),
+                bag_len.T,
+                jnp.transpose(lookup_slot, (1, 2, 0)),
+                slot_row.reshape(groups, per_peer).T,
+                accum,
+            )
+        )
     )
     chunk = min(rows, 128)
     return pl.pallas_call(

time: 22.2 us -> 20.8 us (0.937)
  local copies, waits for them, and re-layouts: 0.76 us -> 0.01 us
  Pallas kernels: 20.6 us -> 20 us
    unnamed x4 -> x2, local copies, waits for them, and re-layouts: 0.76 us -> 0.01 us
    pallas_call x1, Pallas kernels: 19.3 us -> 18.7 us  [per_device(): pl.pallas_call(functools.partial(kernel, groups, lanes, place_base, accum...]
where the time goes in v1:
time: 20.8 us; the launch traced here: 20.6 us
  Pallas kernels  20 us (96%)
  between operations  0.66 us (3%)
    pallas_call x1, Pallas kernels, per_device(): pl.pallas_call(functools.partial(kernel, groups, lanes, place_base, accum...  18.7 us
    pallas_call x1, Pallas kernels, per_device(): pl.pallas_call(functools.partial(update_kernel, chunk, slots, place_base,...  1.28 us

profile of v1, /device:TPU:0, one launch (start us, length us, event | category | flops | bytes accessed | tf_op | source)
XLA Modules:
  0.0 20.6 jit_solution(2348072099422690957)
XLA Ops:
  0.6 0.0 copy-start
  0.6 18.7 %shard_map.77.packed = f32[32,256]{1,0:T(8,128)S(1)} custom-call(bf16[2048,256]{1,0:T(8,128)(2,1)} %bitcast.6, s32[16,128]{1,0:T(8,128)} %bitcast.8, s32[4,8,512]{2,1,0:T(8,128)} %bitcast.7, s32[2,8]{1,0:T(2,128)} %bitcast.9, f32[4,256]{1,0:T(4,128)} %accum_hbm.1), custom_call_target="tpu_custom_call" | custom-call | flops 67108864 | bytes 16777216 | tf_op jit(solution)/shard_map/pallas_call | solution.py:322
  19.3 0.0 copy-done
  19.4 1.3 %shard_map.78 = (f32[4,256,256]{2,1,0:T(8,128)}, f32[4,256]{1,0:T(4,128)}) custom-call(f32[4,256,256]{2,1,0:T(8,128)S(1)} %copy-done, f32[32,256]{1,0:T(8,128)S(1)} %shard_map.77.packed), custom_call_target="tpu_custom_call" | custom-call | tf_op jit(solution)/shard_map/pallas_call | solution.py:372
Async XLA Ops:
  0.6 18.7 %copy-start = (f32[4,256,256]{2,1,0:T(8,128)S(1)}, f32[4,256,256]{2,1,0:T(8,128)}, u32[]{:S(2)}) copy-start(f32[4,256,256]{2,1,0:T(8,128)} %weights.1) | copy-start | bytes 3145732

commit v2 on v1

--- a/solution.py
+++ b/solution.py
@@ -65,6 +65,14 @@
     b_recv,
     c_send,
     c_recv,
+    near_ready,
+    far_ready,
+    shadow_in,
+    shadow_slot,
+    d_send,
+    d_recv,
+    e_send,
+    e_recv,
 ):
     devices = groups * lanes
     per_peer, embed = recv.shape[1], recv.shape[2]
@@ -105,27 +113,24 @@
         both = jnp.dot(factors, values, preferred_element_type=F32)
         return both[:slots] + both[slots:]
 
+    span = groups // 4
+    near = groups - span
+    is_far = grp >= near
+    is_shadow = (grp >= near - span) & (grp < near)
+
     barrier = pltpu.get_barrier_semaphore()
-
-    def greet(i):
-        far = (me + sign * (i + 1) + devices) % devices
-        pl.semaphore_signal(
-            barrier, inc=1, device_id=(far // lanes, far % lanes), device_id_type=MESH
-        )
+    peers = [lane_peer(step, 1) for step in lane_steps]
+
+    def signal(semaphore, g, q):
+        pl.semaphore_signal(semaphore, inc=1, device_id=(g, q), device_id_type=MESH)
 
     look_copies = []
-    for k, step in enumerate(lane_steps):
-        q = lane_peer(step, 1)
+    for k, q in enumerate(peers):
         src = look_hbm.at[:, :, pl.ds(pl.multiple_of(q * batch, batch), batch)]
         look_copies.append(pltpu.make_async_copy(src, marks_in.at[k], look_sem.at[k]))
         look_copies[-1].start()
     grad_copy = pltpu.make_async_copy(grad_hbm, grad_in, load_sem.at[0])
     grad_copy.start()
-    if devices <= 64:
-        for i in range(devices - 1):
-            greet(i)
-    else:
-        each(devices - 1, greet)
     small_copies = [
         pltpu.make_async_copy(len_hbm, len_v, load_sem.at[1]),
         pltpu.make_async_copy(slot_hbm, slot_v, load_sem.at[2]),
@@ -133,107 +138,220 @@
     ]
     for copy in small_copies:
         copy.start()
-    for copy in look_copies:
-        copy.wait()
+
+    with jax.named_scope("signal_up"):
+        for q in peers[1:]:
+            signal(barrier, grp, q)
+
+        @pl.loop(grp + 1, groups)
+        def _(g):
+            signal(barrier, g, lane)
+
+    with jax.named_scope("barrier"):
+        pl.semaphore_wait(barrier, lanes - 1 + grp)
+    with jax.named_scope("signal_down"):
+
+        @pl.when(is_far)
+        def _():
+            @pl.loop(0, grp)
+            def _(g):
+                signal(far_ready, g, lane)
+
+        @pl.when(grp < near)
+        def _():
+            @pl.loop(0, grp)
+            def _(g):
+                signal(near_ready, g, lane)
+
+    with jax.named_scope("look_wait"):
+        for copy in look_copies:
+            copy.wait()
     for k in range(1, lanes):
         marks_out[k - 1] = marks_in[k].astype(F32).astype(marks_out.dtype)
-    pl.semaphore_wait(barrier, devices - 1)
-
     a_copies = []
-    for k, step in enumerate(lane_steps[1:], 1):
+    for k, q in enumerate(peers[1:], 1):
         copy = pltpu.make_async_remote_copy(
             src_ref=marks_out.at[k - 1],
             dst_ref=marks.at[lane],
             send_sem=a_send.at[k - 1],
             recv_sem=a_recv.at[k - 1],
-            device_id=(grp, lane_peer(step, 1)),
+            device_id=(grp, q),
             device_id_type=MESH,
         )
         copy.start()
         a_copies.append(copy)
 
-    grad_copy.wait()
-    for c in range(embed // 128):
-        grad_f32[c] = grad_in[:, c * 128 : (c + 1) * 128].astype(F32)
-    for t in range(tables_all):
+    with jax.named_scope("grad_wait"):
+        grad_copy.wait()
+    with jax.named_scope("grad_turn"):
         for c in range(embed // 128):
-            grad_t[t, :, c * 128 : (c + 1) * 128] = grad_f32[
-                c, pl.ds(t, batch, stride=tables_all), :
-            ].astype(BF16)
+            grad_f32[c] = grad_in[:, c * 128 : (c + 1) * 128].astype(F32)
+        for t in range(tables_all):
+            for c in range(embed // 128):
+                grad_t[t, :, c * 128 : (c + 1) * 128] = grad_f32[
+                    c, pl.ds(t, batch, stride=tables_all), :
+                ].astype(BF16)
     for copy in small_copies:
         copy.wait()
+    slot_copy = pltpu.make_async_remote_copy(
+        src_ref=slot_v,
+        dst_ref=shadow_slot,
+        send_sem=e_send,
+        recv_sem=e_recv,
+        device_id=(jnp.maximum(grp - span, 0), lane),
+        device_id_type=MESH,
+    )
+
+    @pl.when(is_far)
+    def _():
+        slot_copy.start()
 
     marks[lane] = marks_in[0].astype(F32).astype(marks.dtype)
     number = iota((slots, batch), 0).astype(F32)
-    far_first = list(range(1, groups)) + [0]
 
     for k, step in enumerate(lane_steps):
         m = lane_peer(step, -1)
         if k > 0:
-            a_copies[k - 1].wait_recv()
+            with jax.named_scope(f"marks_wait{k}"):
+                a_copies[k - 1].wait_recv()
         total = partial_of(m)
         for p in range(groups):
             part[m, p] = total[p * per_peer : (p + 1) * per_peer].astype(BF16)
 
-        def send(p):
-            pltpu.make_async_remote_copy(
-                src_ref=part.at[m, p],
-                dst_ref=recv.at[me],
-                send_sem=b_send,
-                recv_sem=b_recv,
-                device_id=(p, m),
-                device_id_type=MESH,
-            ).start()
-
-        if groups <= 64:
-            for dp in far_first:
-                if k == 0 and dp == 0:
-                    pltpu.make_async_copy(part.at[m, grp], recv.at[me], b_recv).start()
-                else:
-                    send((grp + sign * dp + groups) % groups)
-        else:
-            each(groups - 1, lambda i: send((grp + i + 1) % groups))
-            if k == 0:
-                pltpu.make_async_copy(part.at[m, grp], recv.at[me], b_recv).start()
-            else:
-                send(grp)
-
-    slot_f = slot_v[...].astype(F32)
+    def send(p, m):
+        pltpu.make_async_remote_copy(
+            src_ref=part.at[m, p],
+            dst_ref=recv.at[me],
+            send_sem=b_send,
+            recv_sem=b_recv,
+            device_id=(p, m),
+            device_id_type=MESH,
+        ).start()
+
+    def send_shadow(p, m):
+        pltpu.make_async_remote_copy(
+            src_ref=part.at[m, p],
+            dst_ref=shadow_in.at[me],
+            send_sem=d_send,
+            recv_sem=d_recv,
+            device_id=(p - span, m),
+            device_id_type=MESH,
+        ).start()
+
+    with jax.named_scope("near_wait"):
+
+        @pl.when(grp < near - 1)
+        def _():
+            pl.semaphore_wait(near_ready, near - 1 - grp)
+
+    with jax.named_scope("near_send"):
+
+        @pl.loop(near, groups)
+        def _(p):
+            for q in peers[1:]:
+                send_shadow(p, q)
+
+            @pl.when(p - span != grp)
+            def _():
+                send_shadow(p, lane)
+
+            @pl.when(p - span == grp)
+            def _():
+                pltpu.make_async_copy(part.at[lane, p], shadow_in.at[me], d_recv).start()
+
+        @pl.loop(0, near)
+        def _(i):
+            p = jnp.where(sign > 0, i, near - 1 - i)
+
+            @pl.when(p != grp)
+            def _():
+                for m in range(lanes):
+                    send(p, m)
+
+        for q in peers[1:]:
+            send(grp, q)
+        pltpu.make_async_copy(part.at[lane, grp], recv.at[me], b_recv).start()
+
+    with jax.named_scope("far_wait"):
+
+        @pl.when(grp < near)
+        def _():
+            pl.semaphore_wait(far_ready, span)
+
+        @pl.when(is_far & (grp < groups - 1))
+        def _():
+            pl.semaphore_wait(far_ready, groups - 1 - grp)
+
+    with jax.named_scope("far_send"):
+
+        @pl.loop(near, groups)
+        def _(p):
+            @pl.when(p != grp)
+            def _():
+                for m in range(lanes):
+                    send(p, m)
+
     which = iota((slots, groups), 0)
-    column_pick = jnp.zeros((slots, groups), F32)
-    for k in range(per_peer):
-        column_pick = jnp.where(which % per_peer == k, slot_f[k : k + 1, :], column_pick)
-    column_pick = jnp.where(which // per_peer == iota((slots, groups), 1), column_pick, 0.0)
-    target_col = jnp.sum(column_pick, axis=1, keepdims=True)
-    i_id, j_id = iota((slots, slots), 0), iota((slots, slots), 1)
+
+    def named_rows(slot_ref):
+        slot_f = slot_ref[...].astype(F32)
+        pick = jnp.zeros((slots, groups), F32)
+        for k in range(per_peer):
+            pick = jnp.where(which % per_peer == k, slot_f[k : k + 1, :], pick)
+        pick = jnp.where(which // per_peer == iota((slots, groups), 1), pick, 0.0)
+        return jnp.sum(pick, axis=1, keepdims=True)
+
+    @pl.when(is_shadow)
+    def _():
+        slot_copy.wait_recv()
+
+    @pl.when(jnp.logical_not(is_shadow))
+    def _():
+        shadow_slot[...] = jnp.zeros(shadow_slot.shape, jnp.int32)
+
+    incoming[slots:, :] = jnp.zeros((slots, embed), F32)
+    own_col = named_rows(slot_v)
+    target_col = jnp.concatenate([own_col, named_rows(shadow_slot) + tables * rows], axis=0)
+    i_id, j_id = iota((2 * slots, 2 * slots), 0), iota((2 * slots, 2 * slots), 1)
     target_row = jnp.sum(jnp.where(i_id == j_id, target_col, 0.0), axis=0, keepdims=True)
     same = target_col == target_row
     first_col = jnp.sum(jnp.where(same & (j_id < i_id), 1.0, 0.0), axis=1, keepdims=True) == 0.0
     first_row = jnp.sum(jnp.where(same & (i_id < j_id), 1.0, 0.0), axis=0, keepdims=True) == 0.0
     place_row = jnp.where(first_row, target_row, -1.0)
-    packed[place_base : place_base + 1, :slots] = place_row
+    packed[place_base : place_base + 1, :slots] = place_row[:, :slots]
     same_w = jnp.where(same, 1.0, 0.0).astype(BF16)
 
     hits = []
     accum_col = jnp.zeros((slots, 1), F32)
     for t in range(tables):
-        hit = target_col == (iota((slots, rows), 1) + t * rows).astype(F32)
+        hit = own_col == (iota((slots, rows), 1) + t * rows).astype(F32)
         hits.append(hit)
         accum_col += jnp.sum(
             jnp.where(hit, accum_v[t : t + 1, :], 0.0), axis=1, keepdims=True
         )
 
-    pltpu.make_async_copy(recv, recv, b_recv).wait()
-    for g in range(groups):
-        group_sum = recv[g * lanes].astype(F32)
-        for q in range(1, lanes):
-            group_sum += recv[g * lanes + q].astype(F32)
-        incoming[g * per_peer : (g + 1) * per_peer, :] = group_sum
-    grads = jnp.dot(same_w, incoming[...].astype(BF16), preferred_element_type=F32)
-    square_col = jnp.sum(grads * grads, axis=1, keepdims=True) * (1.0 / embed)
-    square_first = jnp.where(first_col, square_col, 0.0)
+    def gather(source, base):
+        for g in range(groups):
+            group_sum = source[g * lanes].astype(F32)
+            for q in range(1, lanes):
+                group_sum += source[g * lanes + q].astype(F32)
+            incoming[base + g * per_peer : base + (g + 1) * per_peer, :] = group_sum
+
+    @pl.when(is_shadow)
+    def _():
+        with jax.named_scope("shadow_wait"):
+            pltpu.make_async_copy(shadow_in, shadow_in, d_recv).wait()
+        gather(shadow_in, slots)
+
+    with jax.named_scope("sums_wait"):
+        pltpu.make_async_copy(recv, recv, b_recv).wait()
+    gather(recv, 0)
+    all_grads = jnp.dot(same_w, incoming[...].astype(BF16), preferred_element_type=F32)
+    square_all = jnp.sum(all_grads * all_grads, axis=1, keepdims=True) * (1.0 / embed)
+    square_first = jnp.where(first_col, square_all, 0.0)
     local = embed * jnp.sum(square_first, axis=0, keepdims=True)
     norm_out[...] = jnp.broadcast_to(local, (1, 128))
+    grads, square_col = all_grads[:slots], square_all[:slots]
 
     def tell(far):
         pltpu.make_async_remote_copy(
@@ -245,23 +363,39 @@
             device_id_type=MESH,
         ).start()
 
-    if devices <= 64:
-        for d in range(1, devices):
-            tell((me + sign * d + devices) % devices)
-    else:
-        each(devices - 1, lambda i: tell((me + i + 1) % devices))
-    pltpu.make_async_copy(norm_out, norm_in.at[me], c_recv).start()
+    @pl.when(jnp.logical_not(is_far))
+    def _():
+        if devices <= 64:
+            for d in range(1, devices):
+                tell((me + sign * d + devices) % devices)
+        else:
+            each(devices - 1, lambda i: tell((me + i + 1) % devices))
+        pltpu.make_async_copy(norm_out, norm_in.at[me], c_recv).start()
 
     square_rows = [
-        jnp.sum(jnp.where(hit, square_first, 0.0), axis=0, keepdims=True) for hit in hits
+        jnp.sum(jnp.where(hit, square_first[:slots], 0.0), axis=0, keepdims=True) for hit in hits
     ]
     for copy in a_copies:
         copy.wait_send()
     sent = recv.at[pl.ds(0, devices - 1)]
     pltpu.make_async_copy(sent, sent, b_send).wait()
 
-    pltpu.make_async_copy(norm_in, norm_in, c_recv).wait()
-    norm_total = jnp.sum(norm_in[...], axis=0)[:, :1]
+    def sent_shadows(count):
+        sent = shadow_in.at[pl.ds(0, count)]
+        pltpu.make_async_copy(sent, sent, d_send).wait()
+
+    if span > 0:
+        pl.when(is_shadow)(lambda: sent_shadows(span * lanes - 1))
+        pl.when(jnp.logical_not(is_shadow))(lambda: sent_shadows(span * lanes))
+
+    @pl.when(is_far)
+    def _():
+        slot_copy.wait_send()
+
+    with jax.named_scope("norm_wait"):
+        told = norm_in.at[pl.ds(0, near * lanes)]
+        pltpu.make_async_copy(told, told, c_recv).wait()
+    norm_total = jnp.sum(norm_in[: near * lanes], axis=0)[:, :1]
     clip_limit = 0.5 * math.sqrt(devices * slots * embed)
     clip = clip_limit / jnp.maximum(jnp.sqrt(norm_total), clip_limit)
     for t in range(tables):
@@ -269,8 +403,11 @@
     new_accum_col = accum_col + clip * clip * square_col
     delta = LEARN_RATE * clip * grads / (jnp.sqrt(new_accum_col) + EPSILON)
     packed[:slots, :embed] = delta
-    told = norm_in.at[pl.ds(0, devices - 1)]
-    pltpu.make_async_copy(told, told, c_send).wait()
+
+    @pl.when(jnp.logical_not(is_far))
+    def _():
+        told = norm_in.at[pl.ds(0, devices - 1)]
+        pltpu.make_async_copy(told, told, c_send).wait()
 
 
 def update_kernel(
@@ -341,13 +478,21 @@
             pltpu.VMEM((tables, rows), F32),
             pltpu.VMEM((lanes, groups, per_peer, embed), BF16),
             pltpu.VMEM((devices, per_peer, embed), BF16),
-            pltpu.VMEM((slots, embed), F32),
+            pltpu.VMEM((2 * slots, embed), F32),
             pltpu.VMEM((1, 128), F32),
             pltpu.VMEM((devices, 1, 128), F32),
             pltpu.SemaphoreType.DMA((4,)),
             pltpu.SemaphoreType.DMA((lanes,)),
             pltpu.SemaphoreType.DMA((lanes - 1,)),
             pltpu.SemaphoreType.DMA((lanes - 1,)),
+            pltpu.SemaphoreType.DMA,
+            pltpu.SemaphoreType.DMA,
+            pltpu.SemaphoreType.DMA,
+            pltpu.SemaphoreType.DMA,
+            pltpu.SemaphoreType.REGULAR,
+            pltpu.SemaphoreType.REGULAR,
+            pltpu.VMEM((devices, per_peer, embed), BF16),
+            pltpu.VMEM((per_peer, groups), jnp.int32),
             pltpu.SemaphoreType.DMA,
             pltpu.SemaphoreType.DMA,
             pltpu.SemaphoreType.DMA,

time: 20.8 us -> 18.6 us (0.89)
  Pallas kernels: 20 us -> 17.8 us
    pallas_call x1, Pallas kernels: 18.7 us -> 16.5 us  [per_device(): pl.pallas_call(functools.partial(kernel, groups, lanes, place_base, accum...]
where the time goes in v2:
time: 18.6 us; the launch traced here: 18.4 us
  Pallas kernels  17.8 us (96%)
  between operations  0.66 us (4%)
    pallas_call x1, Pallas kernels, per_device(): pl.pallas_call(functools.partial(kernel, groups, lanes, place_base, accum...  16.5 us
    pallas_call x1, Pallas kernels, per_device(): pl.pallas_call(functools.partial(update_kernel, chunk, slots, place_base,...  1.28 us

profile of v2, /device:TPU:0, one launch (start us, length us, event | category | flops | bytes accessed | tf_op | source)
XLA Modules:
  0.0 18.4 jit_solution(17135788354258142373)
XLA Ops:
  0.6 0.0 copy-start
  0.6 16.5 %shard_map.77.packed = f32[32,256]{1,0:T(8,128)S(1)} custom-call(bf16[2048,256]{1,0:T(8,128)(2,1)} %bitcast.6, s32[16,128]{1,0:T(8,128)} %bitcast.8, s32[4,8,512]{2,1,0:T(8,128)} %bitcast.7, s32[2,8]{1,0:T(2,128)} %bitcast.9, f32[4,256]{1,0:T(4,128)} %accum_hbm.1), custom_call_target="tpu_custom_call" | custom-call | flops 67108864 | bytes 16777216 | tf_op jit(solution)/shard_map/pallas_call | solution.py:459
  17.2 0.0 copy-done
  17.2 1.3 %shard_map.78 = (f32[4,256,256]{2,1,0:T(8,128)}, f32[4,256]{1,0:T(4,128)}) custom-call(f32[4,256,256]{2,1,0:T(8,128)S(1)} %copy-done, f32[32,256]{1,0:T(8,128)S(1)} %shard_map.77.packed), custom_call_target="tpu_custom_call" | custom-call | tf_op jit(solution)/shard_map/pallas_call | solution.py:517
Async XLA Ops:
  0.6 16.5 %copy-start = (f32[4,256,256]{2,1,0:T(8,128)S(1)}, f32[4,256,256]{2,1,0:T(8,128)}, u32[]{:S(2)}) copy-start(f32[4,256,256]{2,1,0:T(8,128)} %weights.1) | copy-start | bytes 3145732

commit v3 on v2

--- a/solution.py
+++ b/solution.py
@@ -42,7 +42,9 @@
     look_hbm,
     slot_hbm,
     accum_hbm,
+    weights_hbm,
     packed,
+    held,
     grad_in,
     grad_f32,
     grad_t,
@@ -52,9 +54,11 @@
     marks_out,
     slot_v,
     accum_v,
+    part_f,
     part,
     recv,
-    incoming,
+    sums,
+    shadow_sums,
     norm_out,
     norm_in,
     load_sem,
@@ -68,14 +72,19 @@
     near_ready,
     far_ready,
     shadow_in,
+    pair_slot,
     shadow_slot,
     d_send,
     d_recv,
     e_send,
     e_recv,
+    f_send,
+    f_recv,
+    g_send,
+    g_recv,
 ):
     devices = groups * lanes
-    per_peer, embed = recv.shape[1], recv.shape[2]
+    per_peer, embed = slot_v.shape[0], grad_t.shape[2]
     slots = groups * per_peer
     tables_all, batch = grad_t.shape[0], grad_t.shape[1]
     tables = tables_all // lanes
@@ -115,8 +124,14 @@
 
     span = groups // 4
     near = groups - span
+    half = lanes // 2
+    column, core = lane // 2, lane % 2
+    leader = core == 1
+    widths = embed // 128
+    tile = recv.shape[1]
     is_far = grp >= near
-    is_shadow = (grp >= near - span) & (grp < near)
+    tells = leader & (grp < near)
+    is_shadow = leader & (grp >= near - span) & (grp < near)
 
     barrier = pltpu.get_barrier_semaphore()
     peers = [lane_peer(step, 1) for step in lane_steps]
@@ -130,14 +145,12 @@
         look_copies.append(pltpu.make_async_copy(src, marks_in.at[k], look_sem.at[k]))
         look_copies[-1].start()
     grad_copy = pltpu.make_async_copy(grad_hbm, grad_in, load_sem.at[0])
-    grad_copy.start()
+    weights_copy = pltpu.make_async_copy(weights_hbm, held, load_sem.at[4])
     small_copies = [
         pltpu.make_async_copy(len_hbm, len_v, load_sem.at[1]),
         pltpu.make_async_copy(slot_hbm, slot_v, load_sem.at[2]),
         pltpu.make_async_copy(accum_hbm, accum_v, load_sem.at[3]),
     ]
-    for copy in small_copies:
-        copy.start()
 
     with jax.named_scope("signal_up"):
         for q in peers[1:]:
@@ -146,6 +159,10 @@
         @pl.loop(grp + 1, groups)
         def _(g):
             signal(barrier, g, lane)
+
+    grad_copy.start()
+    for copy in small_copies:
+        copy.start()
 
     with jax.named_scope("barrier"):
         pl.semaphore_wait(barrier, lanes - 1 + grp)
@@ -183,6 +200,7 @@
 
     with jax.named_scope("grad_wait"):
         grad_copy.wait()
+    weights_copy.start()
     with jax.named_scope("grad_turn"):
         for c in range(embed // 128):
             grad_f32[c] = grad_in[:, c * 128 : (c + 1) * 128].astype(F32)
@@ -193,18 +211,33 @@
                 ].astype(BF16)
     for copy in small_copies:
         copy.wait()
+    pair_copy = pltpu.make_async_remote_copy(
+        src_ref=slot_v,
+        dst_ref=pair_slot,
+        send_sem=e_send,
+        recv_sem=e_recv,
+        device_id=(grp, lane - core + 1),
+        device_id_type=MESH,
+    )
     slot_copy = pltpu.make_async_remote_copy(
         src_ref=slot_v,
-        dst_ref=shadow_slot,
-        send_sem=e_send,
-        recv_sem=e_recv,
-        device_id=(jnp.maximum(grp - span, 0), lane),
+        dst_ref=shadow_slot.at[core],
+        send_sem=f_send,
+        recv_sem=f_recv,
+        device_id=(jnp.maximum(grp - span, 0), lane - core + 1),
         device_id_type=MESH,
     )
 
-    @pl.when(is_far)
-    def _():
-        slot_copy.start()
+    @pl.when(core == 0)
+    def _():
+        pair_copy.start()
+        pair_slot[...] = jnp.zeros(pair_slot.shape, jnp.int32)
+
+    @pl.when(jnp.logical_not(is_shadow))
+    def _():
+        shadow_slot[...] = jnp.zeros(shadow_slot.shape, jnp.int32)
+
+    shadow_sums[...] = jnp.zeros(shadow_sums.shape, BF16)
 
     marks[lane] = marks_in[0].astype(F32).astype(marks.dtype)
     number = iota((slots, batch), 0).astype(F32)
@@ -214,30 +247,44 @@
         if k > 0:
             with jax.named_scope(f"marks_wait{k}"):
                 a_copies[k - 1].wait_recv()
+        if k == 1:
+
+            @pl.when(is_far)
+            def _():
+                slot_copy.start()
+
         total = partial_of(m)
+        for h in range(widths):
+            part_f[m // 2, pl.ds(m % 2 * widths + h, slots, stride=2 * widths), :] = total[
+                :, h * 128 : (h + 1) * 128
+            ]
+    for x in range(half):
         for p in range(groups):
-            part[m, p] = total[p * per_peer : (p + 1) * per_peer].astype(BF16)
-
-    def send(p, m):
+            part[x, p] = part_f[x, p * tile : (p + 1) * tile].astype(BF16)
+
+    def send(p, x):
         pltpu.make_async_remote_copy(
-            src_ref=part.at[m, p],
+            src_ref=part.at[x, p],
             dst_ref=recv.at[me],
             send_sem=b_send,
             recv_sem=b_recv,
-            device_id=(p, m),
+            device_id=(p, 2 * x + 1),
             device_id_type=MESH,
         ).start()
 
-    def send_shadow(p, m):
+    def send_shadow(p, x):
         pltpu.make_async_remote_copy(
-            src_ref=part.at[m, p],
+            src_ref=part.at[x, p],
             dst_ref=shadow_in.at[me],
             send_sem=d_send,
             recv_sem=d_recv,
-            device_id=(p - span, m),
+            device_id=(p - span, 2 * x + 1),
             device_id_type=MESH,
         ).start()
 
+    def mine(p, x):
+        return leader & (p == grp) & (x == column)
+
     with jax.named_scope("near_wait"):
 
         @pl.when(grp < near - 1)
@@ -248,29 +295,29 @@
 
         @pl.loop(near, groups)
         def _(p):
-            for q in peers[1:]:
-                send_shadow(p, q)
-
-            @pl.when(p - span != grp)
-            def _():
-                send_shadow(p, lane)
-
-            @pl.when(p - span == grp)
-            def _():
-                pltpu.make_async_copy(part.at[lane, p], shadow_in.at[me], d_recv).start()
+            for x in range(half):
+                here = mine(p - span, x)
+
+                @pl.when(jnp.logical_not(here))
+                def _():
+                    send_shadow(p, x)
+
+                @pl.when(here)
+                def _():
+                    pltpu.make_async_copy(part.at[x, p], shadow_in.at[me], d_recv).start()
 
         @pl.loop(0, near)
         def _(i):
             p = jnp.where(sign > 0, i, near - 1 - i)
-
-            @pl.when(p != grp)
-            def _():
-                for m in range(lanes):
-                    send(p, m)
-
-        for q in peers[1:]:
-            send(grp, q)
-        pltpu.make_async_copy(part.at[lane, grp], recv.at[me], b_recv).start()
+            for x in range(half):
+
+                @pl.when(jnp.logical_not(mine(p, x)))
+                def _():
+                    send(p, x)
+
+        @pl.when(leader)
+        def _():
+            pltpu.make_async_copy(part.at[column, grp], recv.at[me], b_recv).start()
 
     with jax.named_scope("far_wait"):
 
@@ -286,125 +333,177 @@
 
         @pl.loop(near, groups)
         def _(p):
-            @pl.when(p != grp)
-            def _():
-                for m in range(lanes):
-                    send(p, m)
-
-    which = iota((slots, groups), 0)
-
-    def named_rows(slot_ref):
-        slot_f = slot_ref[...].astype(F32)
-        pick = jnp.zeros((slots, groups), F32)
+            for x in range(half):
+
+                @pl.when(jnp.logical_not(mine(p, x)))
+                def _():
+                    send(p, x)
+
+    two = 2 * slots
+    which = iota((two, groups), 0)
+    span_of = tables * rows
+
+    def named_rows(low, high):
+        low, high = low.astype(F32), high.astype(F32)
+        pick = jnp.zeros((two, groups), F32)
         for k in range(per_peer):
-            pick = jnp.where(which % per_peer == k, slot_f[k : k + 1, :], pick)
-        pick = jnp.where(which // per_peer == iota((slots, groups), 1), pick, 0.0)
+            pick = jnp.where(which % (2 * per_peer) == 2 * k, low[k : k + 1, :], pick)
+            pick = jnp.where(which % (2 * per_peer) == 2 * k + 1, high[k : k + 1, :], pick)
+        pick = jnp.where(which // (2 * per_peer) == iota((two, groups), 1), pick, 0.0)
         return jnp.sum(pick, axis=1, keepdims=True)
 
+    @pl.when(leader)
+    def _():
+        pair_copy.wait_recv()
+
     @pl.when(is_shadow)
     def _():
-        slot_copy.wait_recv()
-
-    @pl.when(jnp.logical_not(is_shadow))
-    def _():
-        shadow_slot[...] = jnp.zeros(shadow_slot.shape, jnp.int32)
-
-    incoming[slots:, :] = jnp.zeros((slots, embed), F32)
-    own_col = named_rows(slot_v)
-    target_col = jnp.concatenate([own_col, named_rows(shadow_slot) + tables * rows], axis=0)
-    i_id, j_id = iota((2 * slots, 2 * slots), 0), iota((2 * slots, 2 * slots), 1)
+        pltpu.make_async_copy(shadow_slot, shadow_slot, f_recv).wait()
+
+    own_slot, other_slot = slot_v[...], pair_slot[...] + span_of
+    target_col = jnp.concatenate(
+        [
+            named_rows(
+                jnp.where(leader, other_slot, own_slot), jnp.where(leader, own_slot, other_slot)
+            ),
+            named_rows(shadow_slot[0] + 2 * span_of, shadow_slot[1] + 3 * span_of),
+        ],
+        axis=0,
+    )
+    i_id, j_id = iota((2 * two, 2 * two), 0), iota((2 * two, 2 * two), 1)
     target_row = jnp.sum(jnp.where(i_id == j_id, target_col, 0.0), axis=0, keepdims=True)
     same = target_col == target_row
     first_col = jnp.sum(jnp.where(same & (j_id < i_id), 1.0, 0.0), axis=1, keepdims=True) == 0.0
     first_row = jnp.sum(jnp.where(same & (i_id < j_id), 1.0, 0.0), axis=0, keepdims=True) == 0.0
-    place_row = jnp.where(first_row, target_row, -1.0)
-    packed[place_base : place_base + 1, :slots] = place_row[:, :slots]
-    same_w = jnp.where(same, 1.0, 0.0).astype(BF16)
+    is_own = (target_row < span_of) & first_row
+    place_row = jnp.where(is_own, target_row, -1.0)
+    packed[place_base : place_base + 1, :two] = place_row[:, :two]
+    wide = (2 * two, widths * 2 * two)
+    wide_i, wide_j = iota(wide, 0), iota(wide, 1)
+    spread_row = jnp.sum(
+        jnp.where(wide_i == wide_j // widths, target_col, 0.0), axis=0, keepdims=True
+    )
+    picks = [
+        jnp.where((target_col == spread_row) & (wide_j % widths == h), 1.0, 0.0).astype(BF16)
+        for h in range(widths)
+    ]
 
     hits = []
-    accum_col = jnp.zeros((slots, 1), F32)
+    accum_col = jnp.zeros((two, 1), F32)
     for t in range(tables):
-        hit = own_col == (iota((slots, rows), 1) + t * rows).astype(F32)
+        hit = target_col[:two] == (iota((two, rows), 1) + t * rows).astype(F32)
         hits.append(hit)
         accum_col += jnp.sum(
             jnp.where(hit, accum_v[t : t + 1, :], 0.0), axis=1, keepdims=True
         )
 
-    def gather(source, base):
+    def gather(source):
+        group_sums = []
         for g in range(groups):
             group_sum = source[g * lanes].astype(F32)
             for q in range(1, lanes):
                 group_sum += source[g * lanes + q].astype(F32)
-            incoming[base + g * per_peer : base + (g + 1) * per_peer, :] = group_sum
+            group_sums.append(group_sum)
+        return jnp.concatenate(group_sums, axis=0).astype(BF16)
+
+    sums_copy = pltpu.make_async_remote_copy(
+        src_ref=sums,
+        dst_ref=sums,
+        send_sem=g_send,
+        recv_sem=g_recv,
+        device_id=(grp, lane - core),
+        device_id_type=MESH,
+    )
 
     @pl.when(is_shadow)
     def _():
         with jax.named_scope("shadow_wait"):
             pltpu.make_async_copy(shadow_in, shadow_in, d_recv).wait()
-        gather(shadow_in, slots)
+        shadow_sums[...] = gather(shadow_in)
 
     with jax.named_scope("sums_wait"):
-        pltpu.make_async_copy(recv, recv, b_recv).wait()
-    gather(recv, 0)
-    all_grads = jnp.dot(same_w, incoming[...].astype(BF16), preferred_element_type=F32)
-    square_all = jnp.sum(all_grads * all_grads, axis=1, keepdims=True) * (1.0 / embed)
+
+        @pl.when(leader)
+        def _():
+            pltpu.make_async_copy(recv, recv, b_recv).wait()
+            sums[...] = gather(recv)
+            sums_copy.start()
+
+        @pl.when(core == 0)
+        def _():
+            sums_copy.wait_recv()
+
+    all_sums = jnp.concatenate([sums[...], shadow_sums[...]], axis=0)
+    pieces = [jnp.dot(pick, all_sums, preferred_element_type=F32) for pick in picks]
+    square_all = sum(piece * piece for piece in pieces)
+    square_all = jnp.sum(square_all, axis=1, keepdims=True) * (1.0 / embed)
     square_first = jnp.where(first_col, square_all, 0.0)
     local = embed * jnp.sum(square_first, axis=0, keepdims=True)
+    grads = jnp.concatenate([piece[:two] for piece in pieces], axis=1)
+    square_col = square_all[:two]
     norm_out[...] = jnp.broadcast_to(local, (1, 128))
-    grads, square_col = all_grads[:slots], square_all[:slots]
 
     def tell(far):
         pltpu.make_async_remote_copy(
             src_ref=norm_out,
-            dst_ref=norm_in.at[me],
+            dst_ref=norm_in.at[grp * half + column],
             send_sem=c_send,
             recv_sem=c_recv,
             device_id=(far // lanes, far % lanes),
             device_id_type=MESH,
         ).start()
 
-    @pl.when(jnp.logical_not(is_far))
+    @pl.when(tells)
     def _():
         if devices <= 64:
             for d in range(1, devices):
                 tell((me + sign * d + devices) % devices)
         else:
             each(devices - 1, lambda i: tell((me + i + 1) % devices))
-        pltpu.make_async_copy(norm_out, norm_in.at[me], c_recv).start()
+        pltpu.make_async_copy(norm_out, norm_in.at[grp * half + column], c_recv).start()
 
     square_rows = [
-        jnp.sum(jnp.where(hit, square_first[:slots], 0.0), axis=0, keepdims=True) for hit in hits
+        jnp.sum(jnp.where(hit, square_first[:two], 0.0), axis=0, keepdims=True) for hit in hits
     ]
     for copy in a_copies:
         copy.wait_send()
-    sent = recv.at[pl.ds(0, devices - 1)]
-    pltpu.make_async_copy(sent, sent, b_send).wait()
-
-    def sent_shadows(count):
-        sent = shadow_in.at[pl.ds(0, count)]
-        pltpu.make_async_copy(sent, sent, d_send).wait()
-
+
+    def sent(buffer, count, semaphore):
+        piece = buffer.at[pl.ds(0, count)]
+        pltpu.make_async_copy(piece, piece, semaphore).wait()
+
+    pl.when(leader)(lambda: sent(recv, groups * half - 1, b_send))
+    pl.when(core == 0)(lambda: sent(recv, groups * half, b_send))
     if span > 0:
-        pl.when(is_shadow)(lambda: sent_shadows(span * lanes - 1))
-        pl.when(jnp.logical_not(is_shadow))(lambda: sent_shadows(span * lanes))
+        pl.when(is_shadow)(lambda: sent(shadow_in, span * half - 1, d_send))
+        pl.when(jnp.logical_not(is_shadow))(lambda: sent(shadow_in, span * half, d_send))
 
     @pl.when(is_far)
     def _():
         slot_copy.wait_send()
 
+    @pl.when(core == 0)
+    def _():
+        pair_copy.wait_send()
+
+    @pl.when(leader)
+    def _():
+        sums_copy.wait_send()
+
     with jax.named_scope("norm_wait"):
-        told = norm_in.at[pl.ds(0, near * lanes)]
+        told = norm_in.at[pl.ds(0, near * half)]
         pltpu.make_async_copy(told, told, c_recv).wait()
-    norm_total = jnp.sum(norm_in[: near * lanes], axis=0)[:, :1]
+    weights_copy.wait()
+    norm_total = jnp.sum(norm_in[: near * half], axis=0)[:, :1]
     clip_limit = 0.5 * math.sqrt(devices * slots * embed)
     clip = clip_limit / jnp.maximum(jnp.sqrt(norm_total), clip_limit)
     for t in range(tables):
         packed[accum_base + t : accum_base + t + 1, :rows] = accum_v[t : t + 1, :] + clip * clip * square_rows[t]
     new_accum_col = accum_col + clip * clip * square_col
     delta = LEARN_RATE * clip * grads / (jnp.sqrt(new_accum_col) + EPSILON)
-    packed[:slots, :embed] = delta
-
-    @pl.when(jnp.logical_not(is_far))
+    packed[:two, :embed] = delta
+
+    @pl.when(tells)
     def _():
         told = norm_in.at[pl.ds(0, devices - 1)]
         pltpu.make_async_copy(told, told, c_send).wait()
@@ -451,16 +550,21 @@
     devices = groups * lanes
     slots = groups * per_peer
     mark_type = BF16 if slots <= 256 else F32
-    place_base = -(-slots // 8) * 8
+    half = lanes // 2
+    tile = 2 * per_peer * (embed // 128)
+    place_base = -(-2 * slots // 8) * 8
     accum_base = place_base + 8
-    packed_shape = (accum_base + -(-tables // 8) * 8, max(embed, rows, slots))
+    packed_shape = (accum_base + -(-tables // 8) * 8, max(embed, rows, 2 * slots))
     anywhere = pl.BlockSpec(memory_space=pl.ANY)
     vmem = pl.BlockSpec(memory_space=pltpu.VMEM)
-    packed = pl.pallas_call(
+    packed, held = pl.pallas_call(
         functools.partial(kernel, groups, lanes, place_base, accum_base),
-        out_shape=jax.ShapeDtypeStruct(packed_shape, F32),
-        in_specs=[pl.BlockSpec(memory_space=pltpu.HBM)] * 5,
-        out_specs=vmem,
+        out_shape=(
+            jax.ShapeDtypeStruct(packed_shape, F32),
+            jax.ShapeDtypeStruct(weights.shape, F32),
+        ),
+        in_specs=[pl.BlockSpec(memory_space=pltpu.HBM)] * 6,
+        out_specs=(vmem, vmem),
         cost_estimate=pl.CostEstimate(
             flops=8 * slots * batch * tables_all * embed,
             bytes_accessed=32 * batch * tables_all * embed,
@@ -476,12 +580,14 @@
             pltpu.VMEM((lanes - 1, tables, depth, batch), mark_type),
             pltpu.VMEM((per_peer, groups), jnp.int32),
             pltpu.VMEM((tables, rows), F32),
-            pltpu.VMEM((lanes, groups, per_peer, embed), BF16),
-            pltpu.VMEM((devices, per_peer, embed), BF16),
-            pltpu.VMEM((2 * slots, embed), F32),
+            pltpu.VMEM((half, groups * tile, 128), F32),
+            pltpu.VMEM((half, groups, tile, 128), BF16),
+            pltpu.VMEM((devices, tile, 128), BF16),
+            pltpu.VMEM((groups * tile, 128), BF16),
+            pltpu.VMEM((groups * tile, 128), BF16),
             pltpu.VMEM((1, 128), F32),
             pltpu.VMEM((devices, 1, 128), F32),
-            pltpu.SemaphoreType.DMA((4,)),
+            pltpu.SemaphoreType.DMA((5,)),
             pltpu.SemaphoreType.DMA((lanes,)),
             pltpu.SemaphoreType.DMA((lanes - 1,)),
             pltpu.SemaphoreType.DMA((lanes - 1,)),
@@ -491,8 +597,13 @@
             pltpu.SemaphoreType.DMA,
             pltpu.SemaphoreType.REGULAR,
             pltpu.SemaphoreType.REGULAR,
-            pltpu.VMEM((devices, per_peer, embed), BF16),
+            pltpu.VMEM((devices, tile, 128), BF16),
             pltpu.VMEM((per_peer, groups), jnp.int32),
+            pltpu.VMEM((2, per_peer, groups), jnp.int32),
+            pltpu.SemaphoreType.DMA,
+            pltpu.SemaphoreType.DMA,
+            pltpu.SemaphoreType.DMA,
+            pltpu.SemaphoreType.DMA,
             pltpu.SemaphoreType.DMA,
             pltpu.SemaphoreType.DMA,
             pltpu.SemaphoreType.DMA,
@@ -510,12 +621,13 @@
                 jnp.transpose(lookup_slot, (1, 2, 0)),
                 slot_row.reshape(groups, per_peer).T,
                 accum,
+                weights,
             )
         )
     )
     chunk = min(rows, 128)
     return pl.pallas_call(
-        functools.partial(update_kernel, chunk, slots, place_base, accum_base),
+        functools.partial(update_kernel, chunk, 2 * slots, place_base, accum_base),
         out_shape=(
             jax.ShapeDtypeStruct(weights.shape, F32),
             jax.ShapeDtypeStruct(accum.shape, F32),
@@ -529,7 +641,7 @@
             pltpu.SemaphoreType.DMA,
         ],
         compiler_params=pltpu.CompilerParams(vmem_limit_bytes=8 << 20),
-    )(weights, packed)
+    )(held, packed)
 
 
 def solution(mesh):

time: 18.6 us -> 17.8 us (0.957)
  Pallas kernels: 17.8 us -> 17 us
    pallas_call x1, Pallas kernels: 16.5 us -> 15.7 us  [per_device(): pl.pallas_call(functools.partial(kernel, groups, lanes, place_base, accum...]
where the time goes in v3:
time: 17.8 us; the launch traced here: 17.6 us
  Pallas kernels  17 us (96%)
  between operations  0.64 us (4%)
    pallas_call x1, Pallas kernels, per_device(): pl.pallas_call(functools.partial(kernel, groups, lanes, place_base, accum...  15.7 us
    pallas_call x1, Pallas kernels, per_device(): pl.pallas_call(functools.partial(update_kernel, chunk, 2 * slots, place_b...  1.29 us

profile of v3, /device:TPU:0, one launch (start us, length us, event | category | flops | bytes accessed | tf_op | source)
XLA Modules:
  0.0 17.6 jit_solution(2986684415525225523)
XLA Ops:
  0.6 15.7 %shard_map.77 = (f32[48,256]{1,0:T(8,128)S(1)}, f32[4,256,256]{2,1,0:T(8,128)S(1)}) custom-call(bf16[2048,256]{1,0:T(8,128)(2,1)} %bitcast.6, s32[16,128]{1,0:T(8,128)} %bitcast.8, s32[4,8,512]{2,1,0:T(8,128)} %bitcast.7, s32[2,8]{1,0:T(2,128)} %bitcast.9, f32[4,256]{1,0:T(4,128)} %accum_hbm.1, f32[4,256,256]{2,1,0:T(8,128)} %weights_hbm.1), custom_call_target="tpu_custom_call" | custom-call | flops 67108864 | bytes 16777216 | tf_op jit(solution)/shard_map/pallas_call | solution.py:560
  16.3 1.3 %shard_map.78 = (f32[4,256,256]{2,1,0:T(8,128)}, f32[4,256]{1,0:T(4,128)}) custom-call(f32[4,256,256]{2,1,0:T(8,128)S(1)} %get-tuple-element.4.weights, f32[48,256]{1,0:T(8,128)S(1)} %get-tuple-element.5.packed), custom_call_target="tpu_custom_call" | custom-call | tf_op jit(solution)/shard_map/pallas_call | solution.py:629

commit v4 on v3

--- a/solution.py
+++ b/solution.py
@@ -11,6 +11,7 @@
 MESH = pl.DeviceIdType.MESH
 LEARN_RATE = 0.3
 EPSILON = 1e-06
+SIDE = 2
 F32 = jnp.float32
 BF16 = jnp.bfloat16
 
@@ -71,6 +72,7 @@
     c_recv,
     near_ready,
     far_ready,
+    top_ready,
     shadow_in,
     pair_slot,
     shadow_slot,
@@ -95,14 +97,6 @@
     me = grp * lanes + lane
     sign = 2 * (grp // (groups // 2)) - 1
 
-    lane_steps = [(dx, dc) for dx in range(lanes // 2) for dc in range(2)]
-
-    def lane_peer(step, sign):
-        dx, dc = step
-        half = lanes // 2
-        chip = (lane // 2 + sign * dx + half) % half
-        return chip * 2 + (lane % 2 + dc) % 2
-
     def partial_of(m):
         highs, lows = [], []
         for t in range(tables):
@@ -122,19 +116,42 @@
         both = jnp.dot(factors, values, preferred_element_type=F32)
         return both[:slots] + both[slots:]
 
-    span = groups // 4
+    side = SIDE if groups % (4 * SIDE) == 0 else 1
+    depth_all = groups // side
+    span = depth_all // 4 * side
     near = groups - span
+    near_depth = near // side
+    far_depth = depth_all - near_depth
+    row, place = grp // side, grp % side
+    rows_above, places_above = depth_all - row, side - place
+    near_above = jnp.maximum(near_depth - row, 0) * places_above - jnp.where(grp < near, 1, 0)
+    far_above = jnp.minimum(rows_above, far_depth) * places_above - jnp.where(grp < near, 0, 1)
+
+    def is_apart(g):
+        r, p = g // side, g % side
+        return ((r > 0) & (p < side - 1)) | ((r < depth_all - 1) & (p > 0))
+
+
+    def above(g):
+        return (g // side >= row) & (g % side >= place) & (g != grp)
+
+    def below(g):
+        return (g // side <= row) & (g % side <= place) & (g != grp)
+
     half = lanes // 2
     column, core = lane // 2, lane % 2
     leader = core == 1
     widths = embed // 128
     tile = recv.shape[1]
     is_far = grp >= near
+    is_top = leader & (grp == groups - 1)
     tells = leader & (grp < near)
     is_shadow = leader & (grp >= near - span) & (grp < near)
 
     barrier = pltpu.get_barrier_semaphore()
-    peers = [lane_peer(step, 1) for step in lane_steps]
+    partner = lane + 1 - 2 * core
+    others = [lax.rem(column + d, half) for d in range(1, half)]
+    peers = [lane] + [2 * x for x in others] + [2 * x + 1 for x in others] + [partner]
 
     def signal(semaphore, g, q):
         pl.semaphore_signal(semaphore, inc=1, device_id=(g, q), device_id_type=MESH)
@@ -158,27 +175,56 @@
 
         @pl.loop(grp + 1, groups)
         def _(g):
-            signal(barrier, g, lane)
+            @pl.when(above(g))
+            def _():
+                signal(barrier, g, lane)
+
+        @pl.when(grp < groups - 1)
+        def _():
+            for x in range(half):
+
+                @pl.when(lane != 2 * x + 1)
+                def _():
+                    signal(barrier, groups - 1, 2 * x + 1)
 
     grad_copy.start()
     for copy in small_copies:
         copy.start()
 
     with jax.named_scope("barrier"):
-        pl.semaphore_wait(barrier, lanes - 1 + grp)
+
+        @pl.when(is_top)
+        def _():
+            pl.semaphore_wait(barrier, devices - 1)
+
+        @pl.when(jnp.logical_not(is_top))
+        def _():
+            pl.semaphore_wait(barrier, lanes - 2 + (row + 1) * (place + 1))
+
     with jax.named_scope("signal_down"):
 
-        @pl.when(is_far)
-        def _():
-            @pl.loop(0, grp)
-            def _(g):
+        @pl.loop(0, grp)
+        def _(g):
+            @pl.when(below(g) & is_far)
+            def _():
                 signal(far_ready, g, lane)
 
-        @pl.when(grp < near)
-        def _():
-            @pl.loop(0, grp)
-            def _(g):
+            @pl.when(below(g) & (grp < near))
+            def _():
                 signal(near_ready, g, lane)
+
+        if side > 1:
+
+            @pl.when(is_top)
+            def _():
+                @pl.loop(1, groups - 1)
+                def _(i):
+                    g = groups - 1 - i
+
+                    @pl.when(is_apart(g))
+                    def _():
+                        for q in range(lanes):
+                            signal(top_ready, g, q)
 
     with jax.named_scope("look_wait"):
         for copy in look_copies:
@@ -191,7 +237,7 @@
             src_ref=marks_out.at[k - 1],
             dst_ref=marks.at[lane],
             send_sem=a_send.at[k - 1],
-            recv_sem=a_recv.at[k - 1],
+            recv_sem=a_recv.at[lane],
             device_id=(grp, q),
             device_id_type=MESH,
         )
@@ -242,23 +288,18 @@
     marks[lane] = marks_in[0].astype(F32).astype(marks.dtype)
     number = iota((slots, batch), 0).astype(F32)
 
-    for k, step in enumerate(lane_steps):
-        m = lane_peer(step, -1)
-        if k > 0:
-            with jax.named_scope(f"marks_wait{k}"):
-                a_copies[k - 1].wait_recv()
-        if k == 1:
-
-            @pl.when(is_far)
-            def _():
-                slot_copy.start()
-
+    def take(m):
         total = partial_of(m)
         for h in range(widths):
             part_f[m // 2, pl.ds(m % 2 * widths + h, slots, stride=2 * widths), :] = total[
                 :, h * 128 : (h + 1) * 128
             ]
-    for x in range(half):
+
+    def marks_from(m, name):
+        with jax.named_scope(name):
+            pltpu.make_async_copy(marks.at[m], marks.at[m], a_recv.at[m]).wait()
+
+    def settle(x):
         for p in range(groups):
             part[x, p] = part_f[x, p * tile : (p + 1) * tile].astype(BF16)
 
@@ -285,59 +326,126 @@
     def mine(p, x):
         return leader & (p == grp) & (x == column)
 
-    with jax.named_scope("near_wait"):
-
-        @pl.when(grp < near - 1)
-        def _():
-            pl.semaphore_wait(near_ready, near - 1 - grp)
-
-    with jax.named_scope("near_send"):
-
-        @pl.loop(near, groups)
-        def _(p):
+    def each_group(first, last, body):
+        if groups <= 16:
+            for p in range(first, last):
+                body(p)
+        else:
+            pl.loop(first, last)(body)
+
+    def send_all(first, last, wanted):
+        def body(i):
+            p = last - 1 + first - i
             for x in range(half):
+
+                @pl.when(wanted(p) & jnp.logical_not(mine(p, x)))
+                def _():
+                    send(p, x)
+
+        each_group(first, last, body)
+
+    def send_shadows(wanted, columns):
+        def body(p):
+            for x in columns:
                 here = mine(p - span, x)
 
-                @pl.when(jnp.logical_not(here))
+                @pl.when(wanted(p - span) & jnp.logical_not(here))
                 def _():
                     send_shadow(p, x)
 
-                @pl.when(here)
+                @pl.when(wanted(p - span) & here)
                 def _():
                     pltpu.make_async_copy(part.at[x, p], shadow_in.at[me], d_recv).start()
 
-        @pl.loop(0, near)
-        def _(i):
-            p = jnp.where(sign > 0, i, near - 1 - i)
-            for x in range(half):
-
-                @pl.when(jnp.logical_not(mine(p, x)))
-                def _():
-                    send(p, x)
-
+        each_group(near, groups, body)
+
+    def in_line(p):
+        return above(p) | below(p) | (p == grp)
+
+    def off_line(p):
+        return jnp.logical_not(in_line(p))
+
+    def keep_own():
         @pl.when(leader)
         def _():
             pltpu.make_async_copy(part.at[column, grp], recv.at[me], b_recv).start()
 
-    with jax.named_scope("far_wait"):
-
-        @pl.when(grp < near)
+    def near_known():
+        with jax.named_scope("near_wait"):
+
+            @pl.when(near_above > 0)
+            def _():
+                pl.semaphore_wait(near_ready, near_above)
+
+    def far_known():
+        with jax.named_scope("far_wait"):
+
+            @pl.when(far_above > 0)
+            def _():
+                pl.semaphore_wait(far_ready, far_above)
+
+    def rest_known():
+        with jax.named_scope("column_wait"):
+            pl.semaphore_wait(top_ready, half)
+
+    late = grp >= groups // 2
+    take(lane)
+    marks_from(partner, "marks_wait1")
+
+    @pl.when(is_far)
+    def _():
+        slot_copy.start()
+
+    take(partner)
+    settle(column)
+
+    @pl.when(late)
+    def _():
+        near_known()
+        far_known()
+        pl.when(is_apart(grp))(rest_known)
+        send_shadows(lambda p: True, [column])
+
+        def body(p):
+            @pl.when(jnp.logical_not(leader & (p == grp)))
+            def _():
+                send(p, column)
+
+        each_group(0, groups, body)
+        keep_own()
+
+    for x in others:
+        marks_from(2 * x + 1, "marks_wait2")
+        take(2 * x + 1)
+    for x in others:
+        marks_from(2 * x, "marks_wait3")
+        take(2 * x)
+    for x in others:
+        settle(x)
+
+    @pl.when(late)
+    def _():
+        for x in others:
+            each_group(0, groups, lambda p: send(p, x))
+            each_group(near, groups, lambda p: send_shadow(p, x))
+
+    @pl.when(jnp.logical_not(late))
+    def _():
+        near_known()
+        send_shadows(in_line, range(half))
+        send_all(0, near, in_line)
+        keep_own()
+        far_known()
+        send_all(near, groups, in_line)
+
+        @pl.when(is_apart(grp))
         def _():
-            pl.semaphore_wait(far_ready, span)
-
-        @pl.when(is_far & (grp < groups - 1))
-        def _():
-            pl.semaphore_wait(far_ready, groups - 1 - grp)
-
-    with jax.named_scope("far_send"):
-
-        @pl.loop(near, groups)
-        def _(p):
-            for x in range(half):
-
-                @pl.when(jnp.logical_not(mine(p, x)))
-                def _():
-                    send(p, x)
+            rest_known()
+            send_shadows(off_line, range(half))
+            send_all(0, groups, off_line)
+
+    with jax.named_scope("sent"):
+        pass
 
     two = 2 * slots
     which = iota((two, groups), 0)
@@ -435,13 +543,8 @@
 
     all_sums = jnp.concatenate([sums[...], shadow_sums[...]], axis=0)
     pieces = [jnp.dot(pick, all_sums, preferred_element_type=F32) for pick in picks]
-    square_all = sum(piece * piece for piece in pieces)
-    square_all = jnp.sum(square_all, axis=1, keepdims=True) * (1.0 / embed)
-    square_first = jnp.where(first_col, square_all, 0.0)
-    local = embed * jnp.sum(square_first, axis=0, keepdims=True)
-    grads = jnp.concatenate([piece[:two] for piece in pieces], axis=1)
-    square_col = square_all[:two]
-    norm_out[...] = jnp.broadcast_to(local, (1, 128))
+    squares = sum(piece * piece for piece in pieces)
+    norm_out[...] = jnp.sum(jnp.where(first_col, squares, 0.0), axis=0, keepdims=True)
 
     def tell(far):
         pltpu.make_async_remote_copy(
@@ -462,8 +565,11 @@
             each(devices - 1, lambda i: tell((me + i + 1) % devices))
         pltpu.make_async_copy(norm_out, norm_in.at[grp * half + column], c_recv).start()
 
+    grads = jnp.concatenate([piece[:two] for piece in pieces], axis=1)
+    square_col = jnp.sum(squares[:two], axis=1, keepdims=True) * (1.0 / embed)
+    square_first = jnp.where(first_col[:two], square_col, 0.0)
     square_rows = [
-        jnp.sum(jnp.where(hit, square_first[:two], 0.0), axis=0, keepdims=True) for hit in hits
+        jnp.sum(jnp.where(hit, square_first, 0.0), axis=0, keepdims=True) for hit in hits
     ]
     for copy in a_copies:
         copy.wait_send()
@@ -494,7 +600,7 @@
         told = norm_in.at[pl.ds(0, near * half)]
         pltpu.make_async_copy(told, told, c_recv).wait()
     weights_copy.wait()
-    norm_total = jnp.sum(norm_in[: near * half], axis=0)[:, :1]
+    norm_total = jnp.sum(jnp.sum(norm_in[: near * half], axis=0), axis=1, keepdims=True)
     clip_limit = 0.5 * math.sqrt(devices * slots * embed)
     clip = clip_limit / jnp.maximum(jnp.sqrt(norm_total), clip_limit)
     for t in range(tables):
@@ -590,11 +696,12 @@
             pltpu.SemaphoreType.DMA((5,)),
             pltpu.SemaphoreType.DMA((lanes,)),
             pltpu.SemaphoreType.DMA((lanes - 1,)),
-            pltpu.SemaphoreType.DMA((lanes - 1,)),
-            pltpu.SemaphoreType.DMA,
-            pltpu.SemaphoreType.DMA,
-            pltpu.SemaphoreType.DMA,
-            pltpu.SemaphoreType.DMA,
+            pltpu.SemaphoreType.DMA((lanes,)),
+            pltpu.SemaphoreType.DMA,
+            pltpu.SemaphoreType.DMA,
+            pltpu.SemaphoreType.DMA,
+            pltpu.SemaphoreType.DMA,
+            pltpu.SemaphoreType.REGULAR,
             pltpu.SemaphoreType.REGULAR,
             pltpu.SemaphoreType.REGULAR,
             pltpu.VMEM((devices, tile, 128), BF16),

time: 17.8 us -> 16.8 us (0.944)
  Pallas kernels: 17 us -> 16 us
    pallas_call x1, Pallas kernels: 15.7 us -> 14.7 us  [per_device(): pl.pallas_call(functools.partial(kernel, groups, lanes, place_base, accum...]
where the time goes in v4:
time: 16.8 us; the launch traced here: 16.6 us
  Pallas kernels  16 us (95%)
  between operations  0.64 us (4%)
    pallas_call x1, Pallas kernels, per_device(): pl.pallas_call(functools.partial(kernel, groups, lanes, place_base, accum...  14.7 us
    pallas_call x1, Pallas kernels, per_device(): pl.pallas_call(functools.partial(update_kernel, chunk, 2 * slots, place_b...  1.29 us

profile of v4, /device:TPU:0, one launch (start us, length us, event | category | flops | bytes accessed | tf_op | source)
XLA Modules:
  0.0 16.6 jit_solution(15603148979426517338)
XLA Ops:
  0.6 14.7 %shard_map.77 = (f32[48,256]{1,0:T(8,128)S(1)}, f32[4,256,256]{2,1,0:T(8,128)S(1)}) custom-call(bf16[2048,256]{1,0:T(8,128)(2,1)} %bitcast.6, s32[16,128]{1,0:T(8,128)} %bitcast.8, s32[4,8,512]{2,1,0:T(8,128)} %bitcast.7, s32[2,8]{1,0:T(2,128)} %bitcast.9, f32[4,256]{1,0:T(4,128)} %accum_hbm.1, f32[4,256,256]{2,1,0:T(8,128)} %weights_hbm.1), custom_call_target="tpu_custom_call" | custom-call | flops 67108864 | bytes 16777216 | tf_op jit(solution)/shard_map/pallas_call | solution.py:666
  15.3 1.3 %shard_map.78 = (f32[4,256,256]{2,1,0:T(8,128)}, f32[4,256]{1,0:T(4,128)}) custom-call(f32[4,256,256]{2,1,0:T(8,128)S(1)} %get-tuple-element.4.weights, f32[48,256]{1,0:T(8,128)S(1)} %get-tuple-element.5.packed), custom_call_target="tpu_custom_call" | custom-call | tf_op jit(solution)/shard_map/pallas_call | solution.py:736

commit v5 on v4

--- a/solution.py
+++ b/solution.py
@@ -36,8 +36,6 @@
 def kernel(
     groups,
     lanes,
-    place_base,
-    accum_base,
     grad_hbm,
     len_hbm,
     look_hbm,
@@ -46,6 +44,8 @@
     weights_hbm,
     packed,
     held,
+    place_out,
+    delta_out,
     grad_in,
     grad_f32,
     grad_t,
@@ -484,8 +484,11 @@
     first_col = jnp.sum(jnp.where(same & (j_id < i_id), 1.0, 0.0), axis=1, keepdims=True) == 0.0
     first_row = jnp.sum(jnp.where(same & (i_id < j_id), 1.0, 0.0), axis=0, keepdims=True) == 0.0
     is_own = (target_row < span_of) & first_row
-    place_row = jnp.where(is_own, target_row, -1.0)
-    packed[place_base : place_base + 1, :two] = place_row[:, :two]
+    place_row = jnp.where(is_own, target_row, -1.0)[:, :two]
+    place_row = jnp.concatenate([place_row, place_row], axis=1)
+    for r in range(0, span_of, 128):
+        row_id = (iota((128, 1), 0) + r).astype(F32)
+        place_out[r : r + 128] = jnp.where(row_id == place_row, 1.0, 0.0).astype(BF16)
     wide = (2 * two, widths * 2 * two)
     wide_i, wide_j = iota(wide, 0), iota(wide, 1)
     spread_row = jnp.sum(
@@ -558,11 +561,7 @@
 
     @pl.when(tells)
     def _():
-        if devices <= 64:
-            for d in range(1, devices):
-                tell((me + sign * d + devices) % devices)
-        else:
-            each(devices - 1, lambda i: tell((me + i + 1) % devices))
+        each(devices - 1, lambda i: tell(jnp.where(i < me, i, i + 1)))
         pltpu.make_async_copy(norm_out, norm_in.at[grp * half + column], c_recv).start()
 
     grads = jnp.concatenate([piece[:two] for piece in pieces], axis=1)
@@ -601,13 +600,16 @@
         pltpu.make_async_copy(told, told, c_recv).wait()
     weights_copy.wait()
     norm_total = jnp.sum(jnp.sum(norm_in[: near * half], axis=0), axis=1, keepdims=True)
-    clip_limit = 0.5 * math.sqrt(devices * slots * embed)
-    clip = clip_limit / jnp.maximum(jnp.sqrt(norm_total), clip_limit)
+    clip_limit = 0.25 * devices * slots * embed
+    clip_square = clip_limit / jnp.maximum(norm_total, clip_limit)
     for t in range(tables):
-        packed[accum_base + t : accum_base + t + 1, :rows] = accum_v[t : t + 1, :] + clip * clip * square_rows[t]
-    new_accum_col = accum_col + clip * clip * square_col
-    delta = LEARN_RATE * clip * grads / (jnp.sqrt(new_accum_col) + EPSILON)
-    packed[:two, :embed] = delta
+        packed[t : t + 1, :] = accum_v[t : t + 1, :] + clip_square * square_rows[t]
+    new_accum_col = accum_col + clip_square * square_col
+    rate = LEARN_RATE * jnp.sqrt(clip_square) / (jnp.sqrt(new_accum_col) + EPSILON)
+    delta = rate * grads
+    high = delta.astype(BF16)
+    delta_out[:two] = high
+    delta_out[two:] = (delta - high.astype(F32)).astype(BF16)
 
     @pl.when(tells)
     def _():
@@ -615,25 +617,15 @@
         pltpu.make_async_copy(told, told, c_send).wait()
 
 
-def update_kernel(
-    chunk, slots, place_base, accum_base, weights, packed, wout, aout, held, accum, sems, accum_sem
-):
-    accum[...] = packed[accum_base : accum_base + accum.shape[0], : accum.shape[1]]
-    accum_copy = pltpu.make_async_copy(accum, aout, accum_sem)
-    accum_copy.start()
-    delta = packed[:slots, : weights.shape[2]]
-    high = delta.astype(BF16)
-    deltas = jnp.concatenate([high, (delta - high.astype(F32)).astype(BF16)], axis=0)
-    place_row = packed[place_base : place_base + 1, :slots]
-    place_row = jnp.concatenate([place_row, place_row], axis=1)
+def update_kernel(chunk, weights, place, deltas, packed, wout, aout, held, accum, sems, accum_sem):
     tables, rows = weights.shape[0], weights.shape[1]
     copies = []
     for t in range(tables):
         for c in range(0, rows, chunk):
-            row_id = (iota((chunk, 1), 0) + (t * rows + c)).astype(F32)
-            place = jnp.where(row_id == place_row, 1.0, 0.0).astype(BF16)
             held[t, c : c + chunk] = weights[t, c : c + chunk] - jnp.dot(
-                place, deltas, preferred_element_type=F32
+                place[t * rows + c : t * rows + c + chunk],
+                deltas[...],
+                preferred_element_type=F32,
             )
             copies.append(
                 pltpu.make_async_copy(
@@ -643,6 +635,9 @@
                 )
             )
             copies[-1].start()
+    accum[...] = packed[...]
+    accum_copy = pltpu.make_async_copy(accum, aout, accum_sem)
+    accum_copy.start()
     for copy in copies:
         copy.wait()
     accum_copy.wait()
@@ -658,19 +653,18 @@
     mark_type = BF16 if slots <= 256 else F32
     half = lanes // 2
     tile = 2 * per_peer * (embed // 128)
-    place_base = -(-2 * slots // 8) * 8
-    accum_base = place_base + 8
-    packed_shape = (accum_base + -(-tables // 8) * 8, max(embed, rows, 2 * slots))
     anywhere = pl.BlockSpec(memory_space=pl.ANY)
     vmem = pl.BlockSpec(memory_space=pltpu.VMEM)
-    packed, held = pl.pallas_call(
-        functools.partial(kernel, groups, lanes, place_base, accum_base),
+    packed, held, place, deltas = pl.pallas_call(
+        functools.partial(kernel, groups, lanes),
         out_shape=(
-            jax.ShapeDtypeStruct(packed_shape, F32),
+            jax.ShapeDtypeStruct(accum.shape, F32),
             jax.ShapeDtypeStruct(weights.shape, F32),
+            jax.ShapeDtypeStruct((tables * rows, 4 * slots), BF16),
+            jax.ShapeDtypeStruct((4 * slots, embed), BF16),
         ),
         in_specs=[pl.BlockSpec(memory_space=pltpu.HBM)] * 6,
-        out_specs=(vmem, vmem),
+        out_specs=(vmem,) * 4,
         cost_estimate=pl.CostEstimate(
             flops=8 * slots * batch * tables_all * embed,
             bytes_accessed=32 * batch * tables_all * embed,
@@ -734,12 +728,12 @@
     )
     chunk = min(rows, 128)
     return pl.pallas_call(
-        functools.partial(update_kernel, chunk, 2 * slots, place_base, accum_base),
+        functools.partial(update_kernel, chunk),
         out_shape=(
             jax.ShapeDtypeStruct(weights.shape, F32),
             jax.ShapeDtypeStruct(accum.shape, F32),
         ),
-        in_specs=[vmem, vmem],
+        in_specs=[vmem] * 4,
         out_specs=(anywhere, anywhere),
         scratch_shapes=[
             pltpu.VMEM(weights.shape, F32),
@@ -748,7 +742,7 @@
             pltpu.SemaphoreType.DMA,
         ],
         compiler_params=pltpu.CompilerParams(vmem_limit_bytes=8 << 20),
-    )(held, packed)
+    )(held, place, deltas, packed)
 
 
 def solution(mesh):

time: 16.8 us -> 16.6 us (0.988)
  Pallas kernels: 16 us -> 15.8 us
    pallas_call x2, Pallas kernels: 16 us -> 15.8 us  [the longest x1 14.6 us: per_device(): pl.pallas_call(functools.partial(kernel, groups, lanes), out_shape=(jax.S...]
where the time goes in v5:
time: 16.6 us; the launch traced here: 16.4 us
  Pallas kernels  15.8 us (95%)
  between operations  0.64 us (4%)
    pallas_call x1, Pallas kernels, per_device(): pl.pallas_call(functools.partial(kernel, groups, lanes), out_shape=(jax.S...  14.6 us
    pallas_call x1, Pallas kernels, per_device(): pl.pallas_call(functools.partial(update_kernel, chunk), out_shape=(jax.Sh...  1.21 us

profile of v5, /device:TPU:0, one launch (start us, length us, event | category | flops | bytes accessed | tf_op | source)
XLA Modules:
  0.0 16.4 jit_solution(2545576973784205854)
XLA Ops:
  0.6 14.6 %shard_map.77 = (f32[4,256]{1,0:T(4,128)S(1)}, f32[4,256,256]{2,1,0:T(8,128)S(1)}, bf16[1024,64]{1,0:T(8,128)(2,1)S(1)}, bf16[64,256]{1,0:T(8,128)(2,1)S(1)}) custom-call(bf16[2048,256]{1,0:T(8,128)(2,1)} %bitcast.6, s32[16,128]{1,0:T(8,128)} %bitcast.8, s32[4,8,512]{2,1,0:T(8,128)} %bitcast.7, s32[2,8]{1,0:T(2,128)} %bitcast.9, f32[4,256]{1,0:T(4,128)} %accum_hbm.1, ...), custom_call_target="tpu_custom_call" | custom-call | flops 67108864 | bytes 16777216 | tf_op jit(solution)/shard_map/pallas_call | solution.py:658
  15.2 1.2 %shard_map.78 = (f32[4,256,256]{2,1,0:T(8,128)}, f32[4,256]{1,0:T(4,128)}) custom-call(f32[4,256,256]{2,1,0:T(8,128)S(1)} %get-tuple-element.6.weights, bf16[1024,64]{1,0:T(8,128)(2,1)S(1)} %get-tuple-element.7.place, bf16[64,256]{1,0:T(8,128)(2,1)S(1)} %get-tuple-element.8.deltas, f32[4,256]{1,0:T(4,128)S(1)} %get-tuple-element.9.packed), custom_call_target="tpu_custom_call" | custom-call | tf_op jit(solution)/shard_map/pallas_call | solution.py:730

commit v6 on v5

--- a/solution.py
+++ b/solution.py
@@ -73,11 +73,8 @@
     near_ready,
     far_ready,
     top_ready,
-    shadow_in,
     pair_slot,
     shadow_slot,
-    d_send,
-    d_recv,
     e_send,
     e_recv,
     f_send,
@@ -156,18 +153,15 @@
     def signal(semaphore, g, q):
         pl.semaphore_signal(semaphore, inc=1, device_id=(g, q), device_id_type=MESH)
 
-    look_copies = []
-    for k, q in enumerate(peers):
-        src = look_hbm.at[:, :, pl.ds(pl.multiple_of(q * batch, batch), batch)]
-        look_copies.append(pltpu.make_async_copy(src, marks_in.at[k], look_sem.at[k]))
-        look_copies[-1].start()
+    look_copy = pltpu.make_async_copy(look_hbm, marks_in, look_sem)
+    look_copy.start()
     grad_copy = pltpu.make_async_copy(grad_hbm, grad_in, load_sem.at[0])
-    weights_copy = pltpu.make_async_copy(weights_hbm, held, load_sem.at[4])
+    weights_copy = pltpu.make_async_copy(weights_hbm, held, look_sem)
     small_copies = [
         pltpu.make_async_copy(len_hbm, len_v, load_sem.at[1]),
         pltpu.make_async_copy(slot_hbm, slot_v, load_sem.at[2]),
-        pltpu.make_async_copy(accum_hbm, accum_v, load_sem.at[3]),
     ]
+    accum_copy = pltpu.make_async_copy(accum_hbm, accum_v, load_sem.at[2])
 
     with jax.named_scope("signal_up"):
         for q in peers[1:]:
@@ -227,22 +221,23 @@
                             signal(top_ready, g, q)
 
     with jax.named_scope("look_wait"):
-        for copy in look_copies:
-            copy.wait()
-    for k in range(1, lanes):
-        marks_out[k - 1] = marks_in[k].astype(F32).astype(marks_out.dtype)
-    a_copies = []
+        look_copy.wait()
+
+    def marks_for(q):
+        piece = marks_in[:, :, pl.ds(pl.multiple_of(q * batch, batch), batch)]
+        return piece.astype(F32).astype(marks.dtype)
+
+    for k, q in enumerate(peers[1:]):
+        marks_out[k] = marks_for(q)
     for k, q in enumerate(peers[1:], 1):
-        copy = pltpu.make_async_remote_copy(
+        pltpu.make_async_remote_copy(
             src_ref=marks_out.at[k - 1],
             dst_ref=marks.at[lane],
-            send_sem=a_send.at[k - 1],
+            send_sem=a_send,
             recv_sem=a_recv.at[lane],
             device_id=(grp, q),
             device_id_type=MESH,
-        )
-        copy.start()
-        a_copies.append(copy)
+        ).start()
 
     with jax.named_scope("grad_wait"):
         grad_copy.wait()
@@ -257,6 +252,7 @@
                 ].astype(BF16)
     for copy in small_copies:
         copy.wait()
+    accum_copy.start()
     pair_copy = pltpu.make_async_remote_copy(
         src_ref=slot_v,
         dst_ref=pair_slot,
@@ -285,7 +281,7 @@
 
     shadow_sums[...] = jnp.zeros(shadow_sums.shape, BF16)
 
-    marks[lane] = marks_in[0].astype(F32).astype(marks.dtype)
+    marks[lane] = marks_for(lane)
     number = iota((slots, batch), 0).astype(F32)
 
     def take(m):
@@ -316,9 +312,9 @@
     def send_shadow(p, x):
         pltpu.make_async_remote_copy(
             src_ref=part.at[x, p],
-            dst_ref=shadow_in.at[me],
-            send_sem=d_send,
-            recv_sem=d_recv,
+            dst_ref=recv.at[devices + me],
+            send_sem=b_send,
+            recv_sem=b_recv,
             device_id=(p - span, 2 * x + 1),
             device_id_type=MESH,
         ).start()
@@ -355,7 +351,7 @@
 
                 @pl.when(wanted(p - span) & here)
                 def _():
-                    pltpu.make_async_copy(part.at[x, p], shadow_in.at[me], d_recv).start()
+                    pltpu.make_async_copy(part.at[x, p], recv.at[devices + me], b_recv).start()
 
         each_group(near, groups, body)
 
@@ -499,6 +495,7 @@
         for h in range(widths)
     ]
 
+    accum_copy.wait()
     hits = []
     accum_col = jnp.zeros((two, 1), F32)
     for t in range(tables):
@@ -508,12 +505,12 @@
             jnp.where(hit, accum_v[t : t + 1, :], 0.0), axis=1, keepdims=True
         )
 
-    def gather(source):
+    def gather(base):
         group_sums = []
         for g in range(groups):
-            group_sum = source[g * lanes].astype(F32)
+            group_sum = recv[base + g * lanes].astype(F32)
             for q in range(1, lanes):
-                group_sum += source[g * lanes + q].astype(F32)
+                group_sum += recv[base + g * lanes + q].astype(F32)
             group_sums.append(group_sum)
         return jnp.concatenate(group_sums, axis=0).astype(BF16)
 
@@ -526,18 +523,21 @@
         device_id_type=MESH,
     )
 
-    @pl.when(is_shadow)
-    def _():
-        with jax.named_scope("shadow_wait"):
-            pltpu.make_async_copy(shadow_in, shadow_in, d_recv).wait()
-        shadow_sums[...] = gather(shadow_in)
-
     with jax.named_scope("sums_wait"):
 
+        @pl.when(is_shadow)
+        def _():
+            pltpu.make_async_copy(recv, recv, b_recv).wait()
+            shadow_sums[...] = gather(devices)
+
+        @pl.when(leader & jnp.logical_not(is_shadow))
+        def _():
+            came = recv.at[pl.ds(0, devices)]
+            pltpu.make_async_copy(came, came, b_recv).wait()
+
         @pl.when(leader)
         def _():
-            pltpu.make_async_copy(recv, recv, b_recv).wait()
-            sums[...] = gather(recv)
+            sums[...] = gather(0)
             sums_copy.start()
 
         @pl.when(core == 0)
@@ -570,18 +570,17 @@
     square_rows = [
         jnp.sum(jnp.where(hit, square_first, 0.0), axis=0, keepdims=True) for hit in hits
     ]
-    for copy in a_copies:
-        copy.wait_send()
-
-    def sent(buffer, count, semaphore):
-        piece = buffer.at[pl.ds(0, count)]
-        pltpu.make_async_copy(piece, piece, semaphore).wait()
-
-    pl.when(leader)(lambda: sent(recv, groups * half - 1, b_send))
-    pl.when(core == 0)(lambda: sent(recv, groups * half, b_send))
+    pltpu.make_async_copy(marks_out, marks_out, a_send).wait()
+
+    def sent(count):
+        piece = recv.at[pl.ds(0, count)]
+        pltpu.make_async_copy(piece, piece, b_send).wait()
+
+    total_sent = (groups + span) * half
     if span > 0:
-        pl.when(is_shadow)(lambda: sent(shadow_in, span * half - 1, d_send))
-        pl.when(jnp.logical_not(is_shadow))(lambda: sent(shadow_in, span * half, d_send))
+        pl.when(is_shadow)(lambda: sent(total_sent - 2))
+    pl.when(leader & jnp.logical_not(is_shadow))(lambda: sent(total_sent - 1))
+    pl.when(core == 0)(lambda: sent(total_sent))
 
     @pl.when(is_far)
     def _():
@@ -631,15 +630,14 @@
                 pltpu.make_async_copy(
                     held.at[t, pl.ds(c, chunk)],
                     wout.at[t, pl.ds(c, chunk)],
-                    sems.at[len(copies)],
+                    sems,
                 )
             )
             copies[-1].start()
     accum[...] = packed[...]
     accum_copy = pltpu.make_async_copy(accum, aout, accum_sem)
     accum_copy.start()
-    for copy in copies:
-        copy.wait()
+    pltpu.make_async_copy(held, wout, sems).wait()
     accum_copy.wait()
 
 
@@ -676,20 +674,20 @@
             pltpu.VMEM((tables_all, batch, embed), BF16),
             pltpu.VMEM((tables_all, batch), jnp.int32),
             pltpu.VMEM((lanes, tables, depth, batch), mark_type),
-            pltpu.VMEM((lanes, tables, depth, batch), jnp.int32),
+            pltpu.VMEM((tables, depth, samples), jnp.int32),
             pltpu.VMEM((lanes - 1, tables, depth, batch), mark_type),
             pltpu.VMEM((per_peer, groups), jnp.int32),
             pltpu.VMEM((tables, rows), F32),
             pltpu.VMEM((half, groups * tile, 128), F32),
             pltpu.VMEM((half, groups, tile, 128), BF16),
-            pltpu.VMEM((devices, tile, 128), BF16),
+            pltpu.VMEM((2 * devices, tile, 128), BF16),
             pltpu.VMEM((groups * tile, 128), BF16),
             pltpu.VMEM((groups * tile, 128), BF16),
             pltpu.VMEM((1, 128), F32),
             pltpu.VMEM((devices, 1, 128), F32),
-            pltpu.SemaphoreType.DMA((5,)),
-            pltpu.SemaphoreType.DMA((lanes,)),
-            pltpu.SemaphoreType.DMA((lanes - 1,)),
+            pltpu.SemaphoreType.DMA((3,)),
+            pltpu.SemaphoreType.DMA,
+            pltpu.SemaphoreType.DMA,
             pltpu.SemaphoreType.DMA((lanes,)),
             pltpu.SemaphoreType.DMA,
             pltpu.SemaphoreType.DMA,
@@ -698,11 +696,8 @@
             pltpu.SemaphoreType.REGULAR,
             pltpu.SemaphoreType.REGULAR,
             pltpu.SemaphoreType.REGULAR,
-            pltpu.VMEM((devices, tile, 128), BF16),
             pltpu.VMEM((per_peer, groups), jnp.int32),
             pltpu.VMEM((2, per_peer, groups), jnp.int32),
-            pltpu.SemaphoreType.DMA,
-            pltpu.SemaphoreType.DMA,
             pltpu.SemaphoreType.DMA,
             pltpu.SemaphoreType.DMA,
             pltpu.SemaphoreType.DMA,
@@ -738,7 +733,7 @@
         scratch_shapes=[
             pltpu.VMEM(weights.shape, F32),
             pltpu.VMEM(accum.shape, F32),
-            pltpu.SemaphoreType.DMA((tables * (rows // chunk),)),
+            pltpu.SemaphoreType.DMA,
             pltpu.SemaphoreType.DMA,
         ],
         compiler_params=pltpu.CompilerParams(vmem_limit_bytes=8 << 20),

time: 16.6 us -> 16.5 us (level)
  no operation moved by 1% of the time
where the time goes in v6:
time: 16.5 us; the launch traced here: 16.3 us
  Pallas kernels  15.7 us (95%)
  between operations  0.64 us (4%)
    pallas_call x1, Pallas kernels, per_device(): pl.pallas_call(functools.partial(kernel, groups, lanes), out_shape=(jax.S...  14.5 us
    pallas_call x1, Pallas kernels, per_device(): pl.pallas_call(functools.partial(update_kernel, chunk), out_shape=(jax.Sh...  1.15 us

profile of v6, /device:TPU:0, one launch (start us, length us, event | category | flops | bytes accessed | tf_op | source)
XLA Modules:
  0.0 16.3 jit_solution(9245365614210078765)
XLA Ops:
  0.6 14.5 %shard_map.77 = (f32[4,256]{1,0:T(4,128)S(1)}, f32[4,256,256]{2,1,0:T(8,128)S(1)}, bf16[1024,64]{1,0:T(8,128)(2,1)S(1)}, bf16[64,256]{1,0:T(8,128)(2,1)S(1)}) custom-call(bf16[2048,256]{1,0:T(8,128)(2,1)} %bitcast.6, s32[16,128]{1,0:T(8,128)} %bitcast.8, s32[4,8,512]{2,1,0:T(8,128)} %bitcast.7, s32[2,8]{1,0:T(2,128)} %bitcast.9, f32[4,256]{1,0:T(4,128)} %accum_hbm.1, ...), custom_call_target="tpu_custom_call" | custom-call | flops 67108864 | bytes 16777216 | tf_op jit(solution)/shard_map/pallas_call | solution.py:656
  15.2 1.2 %shard_map.78 = (f32[4,256,256]{2,1,0:T(8,128)}, f32[4,256]{1,0:T(4,128)}) custom-call(f32[4,256,256]{2,1,0:T(8,128)S(1)} %get-tuple-element.6.weights, bf16[1024,64]{1,0:T(8,128)(2,1)S(1)} %get-tuple-element.7.place, bf16[64,256]{1,0:T(8,128)(2,1)S(1)} %get-tuple-element.8.deltas, f32[4,256]{1,0:T(4,128)S(1)} %get-tuple-element.9.packed), custom_call_target="tpu_custom_call" | custom-call | tf_op jit(solution)/shard_map/pallas_call | solution.py:725

commit v7 on v6

--- a/solution.py
+++ b/solution.py
@@ -79,8 +79,6 @@
     e_recv,
     f_send,
     f_recv,
-    g_send,
-    g_recv,
 ):
     devices = groups * lanes
     per_peer, embed = slot_v.shape[0], grad_t.shape[2]
@@ -234,7 +232,7 @@
             src_ref=marks_out.at[k - 1],
             dst_ref=marks.at[lane],
             send_sem=a_send,
-            recv_sem=a_recv.at[lane],
+            recv_sem=a_recv.at[lax.rem(lane - q + lanes, lanes) - 1],
             device_id=(grp, q),
             device_id_type=MESH,
         ).start()
@@ -293,7 +291,8 @@
 
     def marks_from(m, name):
         with jax.named_scope(name):
-            pltpu.make_async_copy(marks.at[m], marks.at[m], a_recv.at[m]).wait()
+            slot = lax.rem(m - lane + lanes, lanes) - 1
+            pltpu.make_async_copy(marks.at[m], marks.at[m], a_recv.at[slot]).wait()
 
     def settle(x):
         for p in range(groups):
@@ -517,8 +516,8 @@
     sums_copy = pltpu.make_async_remote_copy(
         src_ref=sums,
         dst_ref=sums,
-        send_sem=g_send,
-        recv_sem=g_recv,
+        send_sem=e_send,
+        recv_sem=e_recv,
         device_id=(grp, lane - core),
         device_id_type=MESH,
     )
@@ -688,7 +687,7 @@
             pltpu.SemaphoreType.DMA((3,)),
             pltpu.SemaphoreType.DMA,
             pltpu.SemaphoreType.DMA,
-            pltpu.SemaphoreType.DMA((lanes,)),
+            pltpu.SemaphoreType.DMA((lanes - 1,)),
             pltpu.SemaphoreType.DMA,
             pltpu.SemaphoreType.DMA,
             pltpu.SemaphoreType.DMA,
@@ -698,8 +697,6 @@
             pltpu.SemaphoreType.REGULAR,
             pltpu.VMEM((per_peer, groups), jnp.int32),
             pltpu.VMEM((2, per_peer, groups), jnp.int32),
-            pltpu.SemaphoreType.DMA,
-            pltpu.SemaphoreType.DMA,
             pltpu.SemaphoreType.DMA,
             pltpu.SemaphoreType.DMA,
             pltpu.SemaphoreType.DMA,

time: 16.5 us -> 16.5 us (level)
  no operation moved by 1% of the time
where the time goes in v7:
time: 16.5 us; the launch traced here: 16.3 us
  Pallas kernels  15.7 us (95%)
  between operations  0.64 us (4%)
    pallas_call x1, Pallas kernels, per_device(): pl.pallas_call(functools.partial(kernel, groups, lanes), out_shape=(jax.S...  14.5 us
    pallas_call x1, Pallas kernels, per_device(): pl.pallas_call(functools.partial(update_kernel, chunk), out_shape=(jax.Sh...  1.15 us

profile of v7, /device:TPU:0, one launch (start us, length us, event | category | flops | bytes accessed | tf_op | source)
XLA Modules:
  0.0 16.3 jit_solution(17467497642224945811)
XLA Ops:
  0.6 14.5 %shard_map.77 = (f32[4,256]{1,0:T(4,128)S(1)}, f32[4,256,256]{2,1,0:T(8,128)S(1)}, bf16[1024,64]{1,0:T(8,128)(2,1)S(1)}, bf16[64,256]{1,0:T(8,128)(2,1)S(1)}) custom-call(bf16[2048,256]{1,0:T(8,128)(2,1)} %bitcast.6, s32[16,128]{1,0:T(8,128)} %bitcast.8, s32[4,8,512]{2,1,0:T(8,128)} %bitcast.7, s32[2,8]{1,0:T(2,128)} %bitcast.9, f32[4,256]{1,0:T(4,128)} %accum_hbm.1, ...), custom_call_target="tpu_custom_call" | custom-call | flops 67108864 | bytes 16777216 | tf_op jit(solution)/shard_map/pallas_call | solution.py:655
  15.2 1.2 %shard_map.78 = (f32[4,256,256]{2,1,0:T(8,128)}, f32[4,256]{1,0:T(4,128)}) custom-call(f32[4,256,256]{2,1,0:T(8,128)S(1)} %get-tuple-element.6.weights, bf16[1024,64]{1,0:T(8,128)(2,1)S(1)} %get-tuple-element.7.place, bf16[64,256]{1,0:T(8,128)(2,1)S(1)} %get-tuple-element.8.deltas, f32[4,256]{1,0:T(4,128)S(1)} %get-tuple-element.9.packed), custom_call_target="tpu_custom_call" | custom-call | tf_op jit(solution)/shard_map/pallas_call | solution.py:722
